TPU v7x, 32 devices: a whole 2x2x4 slice. The times are simulated.
32 devices in a mesh: inst: 2 (over x), dev: 4 (over z), side: 4 (over y, core).
Axes of the slice: x: 2, y: 2, z: 4, core: 2. Of those that a mesh axis runs over, the one named last changes fastest.
Arguments:
- hidden: bfloat16 [256, 2048], P(('inst', 'dev')), parts along dimension 0
- k_cache: bfloat16 [1, 256, 16, 128, 128], P(None, ('inst', 'dev')), parts along dimension 1
- v_cache: bfloat16 [1, 256, 16, 128, 128], P(None, ('inst', 'dev')), parts along dimension 1
- cache_lens: int32 [256], P(('inst', 'dev')), parts along dimension 0
- expert_ids: int32 [1, 256, 4], P(None, ('inst', 'dev')), parts along dimension 1
- route_gates: float32 [1, 256, 4], P(None, ('inst', 'dev')), parts along dimension 1
- attn_gain: float32 [1, 2048], replicated
- ffn_gain: float32 [1, 2048], replicated
- w_q: bfloat16 [1, 2048, 2048], replicated
- w_kv: bfloat16 [1, 2048, 4096], replicated
- w_o: bfloat16 [1, 2048, 2048], replicated
- shared_gate: bfloat16 [1, 2048, 5632], replicated
- shared_up: bfloat16 [1, 2048, 5632], replicated
- shared_down: bfloat16 [1, 5632, 2048], replicated
- w_gate: bfloat16 [1, 60, 2048, 1408], P(None, 'dev')
- w_up: bfloat16 [1, 60, 2048, 1408], P(None, 'dev')
- w_down: bfloat16 [1, 60, 1408, 2048], P(None, 'dev')
Outputs:
- output: bfloat16 [256, 2048], P(('inst', 'dev')), parts along dimension 0
There are 2 independent parts. A program takes and returns all parts, laid end to end along the dimension named above; an argument that names none is the same for every part.
All inputs are finite; a program needn't handle non-finite values.
Results may differ from a plain program's by a relative error of at most 0.0154421.
Values are sent between devices in bfloat16 or wider.
A program may use at most 1.5 GiB of HBM per device.

v0:
```python
import jax
import jax.numpy as jnp
from jax import lax
from jax.sharding import PartitionSpec as P

NORM_EPS = 1e-6
ROPE_BASE = 10000.0


def rms_norm(in_rows, norm_gain):
    rows_f = in_rows.astype(jnp.float32)
    inv_rms = lax.rsqrt(jnp.mean(rows_f * rows_f, axis=-1, keepdims=True) + NORM_EPS)
    return (rows_f * inv_rms * norm_gain).astype(jnp.bfloat16)


def rotate_pos(in_vecs, positions):
    half_dim = in_vecs.shape[-1] // 2
    inv_freq = ROPE_BASE ** (-jnp.arange(half_dim, dtype=jnp.float32) * 2.0 / in_vecs.shape[-1])
    angles = positions.astype(jnp.float32)[:, None] * inv_freq[None, :]
    cosine = jnp.cos(angles)[:, None, :]
    sine_part = jnp.sin(angles)[:, None, :]
    first_half = in_vecs[..., :half_dim]
    second = in_vecs[..., half_dim:]
    return jnp.concatenate([first_half * cosine - second * sine_part, second * cosine + first_half * sine_part], axis=-1)


def attend(in_rows, key_cache, val_cache, lens_blk, w_query, w_keyval, w_out):
    tokens = in_rows.shape[0]
    kv_heads = key_cache.shape[1]
    seq_len = key_cache.shape[2]
    head_dim = key_cache.shape[3]
    q_heads = w_query.shape[1] // head_dim
    groups = q_heads // kv_heads
    q_rows = jnp.dot(in_rows, w_query, preferred_element_type=jnp.float32).astype(jnp.bfloat16)
    fresh_kv = jnp.dot(in_rows, w_keyval, preferred_element_type=jnp.float32).astype(jnp.bfloat16).reshape(tokens, 2, kv_heads, head_dim)
    q_rows = rotate_pos(q_rows.astype(jnp.float32).reshape(tokens, q_heads, head_dim), lens_blk).astype(jnp.bfloat16).reshape(tokens, kv_heads, groups, head_dim)
    new_key = rotate_pos(fresh_kv[:, 0].astype(jnp.float32), lens_blk).astype(jnp.bfloat16)
    new_val = fresh_kv[:, 1]
    score_scale = head_dim ** -0.5
    scores = jnp.einsum('tkgd,tksd->tkgs', q_rows, key_cache, preferred_element_type=jnp.float32) * score_scale
    valid_mask = jnp.arange(seq_len)[None, None, None, :] < lens_blk[:, None, None, None]
    scores = jnp.where(valid_mask, scores, -jnp.inf)
    self_score = jnp.einsum('tkgd,tkd->tkg', q_rows, new_key, preferred_element_type=jnp.float32) * score_scale
    peak_score = jnp.maximum(jnp.max(scores, axis=-1), self_score)
    weights = jnp.exp(scores - peak_score[..., None])
    self_weight = jnp.exp(self_score - peak_score)
    denom_sum = jnp.sum(weights, axis=-1) + self_weight
    prob_bf = (weights / denom_sum[..., None]).astype(jnp.bfloat16)
    self_prob = (self_weight / denom_sum).astype(jnp.bfloat16)
    context = jnp.einsum('tkgs,tksd->tkgd', prob_bf, val_cache, preferred_element_type=jnp.float32)
    context = context + self_prob.astype(jnp.float32)[..., None] * new_val.astype(jnp.float32)[:, :, None, :]
    context = context.astype(jnp.bfloat16).reshape(tokens, q_heads * head_dim)
    return jnp.dot(context, w_out, preferred_element_type=jnp.float32)


def dense_swiglu(in_rows, gate_w, up_w, down_w):
    act_gate = jnp.dot(in_rows, gate_w, preferred_element_type=jnp.float32)
    act_up = jnp.dot(in_rows, up_w, preferred_element_type=jnp.float32)
    inner_act = (jax.nn.silu(act_gate) * act_up).astype(jnp.bfloat16)
    return jnp.dot(inner_act, down_w, preferred_element_type=jnp.float32).astype(jnp.bfloat16)


def expert_swiglu(in_rows, gate_w, up_w, down_w):
    act_gate = jnp.einsum('secd,edf->secf', in_rows, gate_w, preferred_element_type=jnp.float32)
    act_up = jnp.einsum('secd,edf->secf', in_rows, up_w, preferred_element_type=jnp.float32)
    inner_act = (jax.nn.silu(act_gate) * act_up).astype(jnp.bfloat16)
    return jnp.einsum('secf,efd->secd', inner_act, down_w, preferred_element_type=jnp.float32).astype(jnp.bfloat16)


def capacity_of(block_rows, top_k, num_experts):
    per_block = block_rows * top_k
    return 2 * (per_block // num_experts) - 1 + min(1, per_block % num_experts)


def slot_of(ids_blk, num_experts):
    tokens, top_k = ids_blk.shape
    flat_ids = ids_blk.reshape(tokens * top_k)
    onehot = (flat_ids[:, None] == jnp.arange(num_experts)[None, :]).astype(jnp.int32)
    before = jnp.cumsum(onehot, axis=0) - onehot
    return jnp.sum(before * onehot, axis=1).reshape(tokens, top_k)


def gather_rows(in_rows, ids_blk, slot_blk, num_experts, capacity):
    tokens = in_rows.shape[0]
    expert_hit = (ids_blk[:, :, None] == jnp.arange(num_experts)[None, None, :]).astype(jnp.float32)
    slot_hit = (slot_blk[:, :, None] == jnp.arange(capacity)[None, None, :]).astype(jnp.float32)
    row_index = jnp.arange(tokens, dtype=jnp.float32)[:, None, None] * slot_hit
    owner_idx = jnp.einsum('tje,tjc->ec', expert_hit, row_index, precision=lax.Precision.HIGHEST)
    filled = jnp.einsum('tje,tjc->ec', expert_hit, slot_hit, precision=lax.Precision.HIGHEST)
    picked = jnp.take(in_rows, owner_idx.astype(jnp.int32), axis=0)
    return jnp.where(filled[:, :, None] > 0.5, picked, jnp.zeros_like(picked))


def combine_rows(expert_res, ids_blk, slot_blk, gates_blk):
    num_experts, capacity, model_dim = expert_res.shape
    flat_res = expert_res.reshape(num_experts * capacity, model_dim)
    picked = jnp.take(flat_res, ids_blk * capacity + slot_blk, axis=0)
    return jnp.sum(gates_blk[:, :, None] * picked.astype(jnp.float32), axis=1)


def solution(mesh):
    num_dev = mesh.shape['dev']
    half_side = mesh.shape['side'] // 2
    batch_spec = P(('inst', 'dev'))
    layer_batch = P(None, ('inst', 'dev'))
    expert_spec = P(None, 'dev')
    to_expert = [(column, column + half_side) for column in range(half_side)]
    to_attn = [(column + half_side, column) for column in range(half_side)]

    def device_fn(hidden, k_cache, v_cache, cache_lens, expert_ids, route_gates, attn_gain, ffn_gain, w_q, w_kv, w_o, shared_gate, shared_up, shared_down, w_gate, w_up, w_down):
        side_idx = lax.axis_index('side')
        is_attn = side_idx < half_side
        block_rows = hidden.shape[0] // half_side
        model_dim = hidden.shape[1]
        top_k = expert_ids.shape[2]
        local_experts = w_gate.shape[1]
        num_experts = local_experts * num_dev
        capacity = capacity_of(block_rows, top_k, num_experts)
        row_start = (side_idx % half_side) * block_rows
        x_state = lax.dynamic_slice_in_dim(hidden, row_start, block_rows, axis=0)
        lens_blk = lax.dynamic_slice_in_dim(cache_lens, row_start, block_rows, axis=0)

        def attn_stage(layer_ops):
            cur_rows, key_blk, val_blk, ids_blk, slot_blk, gain_a, gain_f, wq_l, wkv_l, wo_l, sg_l, su_l, sd_l = layer_ops
            normed = rms_norm(cur_rows, gain_a)
            mid_rows = (cur_rows.astype(jnp.float32) + attend(normed, key_blk, val_blk, lens_blk, wq_l, wkv_l, wo_l)).astype(jnp.bfloat16)
            ffn_in = rms_norm(mid_rows, gain_f)
            base_sum = mid_rows.astype(jnp.float32) + dense_swiglu(ffn_in, sg_l, su_l, sd_l).astype(jnp.float32)
            return base_sum, gather_rows(ffn_in, ids_blk, slot_blk, num_experts, capacity)

        def attn_skip(layer_ops):
            return jnp.zeros((block_rows, model_dim), jnp.float32), jnp.zeros((num_experts, capacity, model_dim), jnp.bfloat16)

        def expert_stage(expert_ops):
            return expert_swiglu(expert_ops[0], expert_ops[1], expert_ops[2], expert_ops[3])

        def expert_skip(expert_ops):
            return jnp.zeros_like(expert_ops[0])

        for layer_idx in range(k_cache.shape[0]):
            ids_blk = lax.dynamic_slice_in_dim(expert_ids[layer_idx], row_start, block_rows, axis=0)
            gates_blk = lax.dynamic_slice_in_dim(route_gates[layer_idx], row_start, block_rows, axis=0)
            slot_blk = slot_of(ids_blk, num_experts)
            key_blk = lax.dynamic_slice_in_dim(k_cache[layer_idx], row_start, block_rows, axis=0)
            val_blk = lax.dynamic_slice_in_dim(v_cache[layer_idx], row_start, block_rows, axis=0)
            layer_ops = (x_state, key_blk, val_blk, ids_blk, slot_blk, attn_gain[layer_idx], ffn_gain[layer_idx], w_q[layer_idx], w_kv[layer_idx], w_o[layer_idx], shared_gate[layer_idx], shared_up[layer_idx], shared_down[layer_idx])
            base_sum, send_buf = lax.cond(is_attn, attn_stage, attn_skip, layer_ops)
            spread = lax.all_to_all(send_buf.reshape(num_dev, local_experts, capacity, model_dim), 'dev', 0, 0)
            arrived = lax.ppermute(spread, 'side', to_expert)
            expert_res = lax.cond(is_attn, expert_skip, expert_stage, (arrived, w_gate[layer_idx], w_up[layer_idx], w_down[layer_idx]))
            back_buf = lax.ppermute(expert_res, 'side', to_attn)
            returned = lax.all_to_all(back_buf, 'dev', 0, 0).reshape(num_experts, capacity, model_dim)
            x_state = (base_sum + combine_rows(returned, ids_blk, slot_blk, gates_blk)).astype(jnp.bfloat16)
        gathered = lax.all_gather(x_state, 'side')
        return gathered[:half_side].reshape(half_side * block_rows, model_dim)

    in_specs = (batch_spec, layer_batch, layer_batch, batch_spec, layer_batch, layer_batch, P(), P(), P(), P(), P(), P(), P(), P(), expert_spec, expert_spec, expert_spec)
    return jax.shard_map(device_fn, mesh=mesh, in_specs=in_specs, out_specs=batch_spec, check_vma=False)
```

profile of v0, /device:TPU:0, one launch (start us, length us, event | category | flops | bytes accessed | tf_op | source)
XLA Modules:
  0.0 211.8 jit_solution(4315851330087694244)
XLA Ops:
  0.0 0.8 fusion.139
  0.8 0.8 constant_dynamic-slice_fusion
  1.5 0.1 copy.76
  1.6 0.1 eq.55
  1.7 0.1 fusion.135
  1.8 0.1 reduce_window_sum.11
  1.9 0.2 select_reduce_fusion
  2.1 55.7 %conditional.2 = (f32[16,2048]{1,0:T(8,128)S(1)}, bf16[60,2,2048]{2,1,0:T(2,128)(2,1)S(1)}) conditional(s32[]{:T(128)} %convert_element_type.139, () %tuple.23, (bf16[32,2048]{1,0:T(8,128)(2,1)}, s32[]{:T(128)}, s32[32]{0:T(128)}, f32[1,2048]{1,0:T(1,128)}, bf16[1,2048,2048]{2,1,0:T(8,128)(2,1)}, /*index=5*/bf16[1,32,16,128,128]{4,3,2,1,0:T(8,128)(2,1)}, ...), branch_computations={%region_2.3_spmd, %region_3.8_spmd} | conditional | flops 1664261632 | bytes 222049648 | solution.py:147
  2.1 1.2 fusion.105
  3.3 8.3 %fusion.92 = bf16[2,8,32,128]{3,1,2,0:T(8,128)(2,1)S(1)} fusion(bf16[1,2048,4096]{2,1,0:T(8,128)(2,1)} %get-tuple-element.174, f32[2048]{0:T(1024)} %bitcast.186, f32[16]{0:T(128)S(1)} %add_rsqrt_fusion.1, bf16[32,2048]{1,0:T(8,128)(2,1)} %get-tuple-element.169, s32[]{:T(128)} %get-tuple-element.135), kind=kOutput, calls=%fused_computation.52 | convolution fusion | flops 268632064 | bytes 16982592 | tf_op jit(solution)/shard_map/cond/branch_1_fun/dot_general | solution.py:35
  11.7 0.1 fusion.136
  11.8 0.1 multiply_cosine_fusion
  12.0 1.2 fusion.89
  13.3 0.2 subtract_convert_fusion
  13.4 0.1 fusion.121
  13.6 8.6 %fusion.50 = f32[16,16,1,128]{3,2,1,0:T(1,128)S(1)} fusion(bf16[1,32,16,128,128]{4,3,2,1,0:T(8,128)(2,1)} %get-tuple-element.173, s32[]{:T(128)} %get-tuple-element.135, bf16[16,16,128,1]{2,1,0,3:T(8,128)(2,1)S(1)} %fusion.121), kind=kOutput, calls=%fused_computation.34 | convolution fusion | flops 8388608 | bytes 8585728 | tf_op jit(solution)/shard_map/cond/branch_1_fun/tkgd,tksd->tkgs/dot_general | solution.py:40
  22.1 0.1 iota_compare_fusion.3
  22.2 0.3 fusion.110
  22.5 0.2 fusion.114
  22.7 0.1 fusion.118
  22.9 5.8 %fusion.48 = f32[16,16,1,128]{3,2,1,0:T(1,128)S(1)} fusion(bf16[1,32,16,128,128]{4,3,2,1,0:T(8,128)(2,1)} %get-tuple-element.175, s32[]{:T(128)} %get-tuple-element.135, bf16[16,16,128,1]{2,1,0,3:T(8,128)(2,1)S(1)} %fusion.118), kind=kOutput, calls=%fused_computation.32 | convolution fusion | flops 8388608 | bytes 8585728 | tf_op jit(solution)/shard_map/cond/branch_1_fun/tkgs,tksd->tkgd/dot_general | solution.py:50
  28.7 0.1 fusion.109
  28.8 4.8 %multiply_reduce_fusion = (f32[16]{0:T(128)S(1)}, f32[16,2048]{1,0:T(8,128)S(1)}) fusion(bf16[1,2048,2048]{2,1,0:T(8,128)(2,1)} %get-tuple-element.176, bf16[2,8,16,128]{3,2,1,0:T(8,128)(2,1)S(1)} %bitcast.188, bf16[32,2048]{1,0:T(8,128)(2,1)S(1)} %copy-done.1, s32[]{:T(128)} %get-tuple-element.135), kind=kOutput, calls=%fused_computation.78 | convolution fusion | flops 134414320 | bytes 8650820 | tf_op jit(solution)/shard_map/cond/branch_1_fun/dot_general | solution.py:53
  33.7 0.1 multiply_convert_fusion
  33.8 3.1 %fusion.42 = f32[16,5632]{1,0:T(8,128)S(1)} fusion(bf16[16,2048]{1,0:T(8,128)(2,1)S(1)} %multiply_convert_fusion, bf16[1,2048,5632]{2,1,0:T(8,128)(2,1)S(1)} %bitcast.175), kind=kOutput, calls=%fused_computation.26 | convolution fusion | flops 369098752 | bytes 23494656 | tf_op jit(solution)/shard_map/cond/branch_1_fun/dot_general | solution.py:57
  36.9 17.5 %fusion.86 = f32[16,2048]{1,0:T(8,128)S(1)} fusion(f32[16,2048]{1,0:T(8,128)S(1)} %get-tuple-element.212, bf16[1,5632,2048]{2,1,0:T(8,128)(2,1)} %get-tuple-element.180, bf16[16,2048]{1,0:T(8,128)(2,1)S(1)} %multiply_convert_fusion, bf16[1,2048,5632]{2,1,0:T(8,128)(2,1)} %get-tuple-element.179, f32[16,5632]{1,0:T(8,128)S(1)} %fusion.42), kind=kOutput, calls=%fused_computation.50 | convolution fusion | flops 738836480 | bytes 46825472 | tf_op jit(solution)/shard_map/cond/branch_1_fun/dot_general | solution.py:60
  54.4 0.1 eq.47
  54.5 0.1 copy.72
  54.6 0.2 fusion.96
  54.8 0.1 copy.73
  54.9 0.2 compare_and_fusion
  55.1 0.1 copy.75
  55.2 0.1 reshape.253
  55.4 0.9 gather_fusion
  56.3 0.3 reshape.252
  56.6 0.1 copy.74
  56.8 0.8 broadcast_select_fusion.1
  57.7 19.9 %all_to_all.10 = bf16[4,15,2,2048]{3,2,1,0:T(2,128)(2,1)S(1)} all-to-all(bf16[4,15,2,2048]{3,2,1,0:T(2,128)(2,1)S(1)} %bitcast.181), channel_id=1, replica_groups=mesh['inst'=2,'dev'=4,'side'=4] {'dev'}, dimensions={0} | all-to-all | bytes 983040 | tf_op jit(solution)/shard_map/all_to_all | solution.py:148
  77.7 1.3 collective-permute-start
  79.0 9.7 %collective-permute-done = bf16[4,15,2,2048]{3,2,1,0:T(2,128)(2,1)S(1)} collective-permute-done((bf16[4,15,2,2048]{3,2,1,0:T(2,128)(2,1)S(1)}, bf16[4,15,2,2048]{3,2,1,0:T(2,128)(2,1)S(1)}, u32[]{:S(2)}, u32[]{:S(2)}) %collective-permute-start) | collective-permute-done | bytes 491552 | tf_op jit(solution)/shard_map/ppermute | solution.py:149
  88.7 0.2 conditional.3
  88.7 0.2 broadcast.212
  88.9 0.5 copy.81
  89.4 1.3 collective-permute-start.1
  90.7 97.3 %collective-permute-done.1 = bf16[4,15,2,2048]{3,2,1,0:T(2,128)(2,1)} collective-permute-done((bf16[4,15,2,2048]{3,2,1,0:T(2,128)(2,1)S(1)}, bf16[4,15,2,2048]{3,2,1,0:T(2,128)(2,1)}, u32[]{:S(2)}, u32[]{:S(2)}) %collective-permute-start.1) | collective-permute-done | bytes 491552 | tf_op jit(solution)/shard_map/ppermute | solution.py:151
  188.0 3.8 %all-to-all-start.1 = ((bf16[4,15,2,2048]{3,2,1,0:T(2,128)(2,1)}), bf16[4,15,2,2048]{3,2,1,0:T(2,128)(2,1)S(1)}, u32[]{:S(2)}, u32[]{:S(2)}) async-start(bf16[4,15,2,2048]{3,2,1,0:T(2,128)(2,1)} %collective-permute-done.1), calls=%async_computation.1 | async-start | bytes 983040 | tf_op jit(solution)/shard_map/all_to_all | solution.py:152
  191.8 0.1 reshape.245
  191.9 0.1 reshape.243
  192.0 0.1 copy.82
  192.1 0.1 compare_select_fusion.1
  192.1 0.1 copy.83
  192.2 0.1 reshape.261
  192.3 0.1 dynamic-slice_bitcast_fusion
  192.4 0.1 copy.77
  192.5 0.1 copy.78
  192.6 0.1 compare_and_fusion.1
  192.7 0.1 copy.79
  192.8 10.9 %all-to-all-done.1 = bf16[4,15,2,2048]{3,2,1,0:T(2,128)(2,1)S(1)} async-done(((bf16[4,15,2,2048]{3,2,1,0:T(2,128)(2,1)}), bf16[4,15,2,2048]{3,2,1,0:T(2,128)(2,1)S(1)}, u32[]{:S(2)}, u32[]{:S(2)}) %all-to-all-start.1) | async-done | bytes 491552 | tf_op jit(solution)/shard_map/all_to_all | solution.py:152
  203.7 0.2 reshape_reshape.3
  203.9 0.7 gather_fusion.1
  204.7 0.1 reshape.260
  204.8 0.6 multiply_reduce_fusion.1
  205.4 5.8 %all-gather = bf16[64,2048]{1,0:T(8,128)(2,1)S(1)} all-gather(bf16[16,2048]{1,0:T(8,128)(2,1)S(1)} %add_convert_fusion.2), channel_id=2, replica_groups=mesh['inst'=2,'dev'=4,'side'=4] {'side'}, dimensions={0}, use_global_device_ids=true | all-gather | bytes 327680 | tf_op jit(solution)/shard_map/all_gather | solution.py:154
  211.1 0.7 slice.45
  (41 shorter events, 0.2 us)
Async XLA Ops:
  0.0 192.3 %copy-start = (f32[1,32,4]{1,2,0:T(4,128)S(1)}, f32[1,32,4]{1,2,0:T(4,128)}, u32[]{:S(2)}) copy-start(f32[1,32,4]{1,2,0:T(4,128)} %param.26) | copy-start | bytes 1540
  2.1 9.7 %copy-start.5 = (s32[32]{0:T(128)S(1)}, s32[32]{0:T(128)}, u32[]{:S(2)}) copy-start(s32[32]{0:T(128)} %get-tuple-element.170) | copy-start | bytes 388 | tf_op jit(solution)/shard_map/cond
  2.1 9.9 %slice-start.6 = ((s8[8388608]{0:T(1024)(128)(4,1)}), s8[4194304]{0:T(1024)(128)(4,1)S(1)}, s32[]{:S(2)}) async-start(s8[8388608]{0:T(1024)(128)(4,1)} %bitcast.176), calls=%async_computation.8 | async-start | bytes 8388608 | tf_op jit(solution)/shard_map/cond
  2.1 9.8 %copy-start.1 = (bf16[32,2048]{1,0:T(8,128)(2,1)S(1)}, bf16[32,2048]{1,0:T(8,128)(2,1)}, u32[]{:S(2)}) copy-start(bf16[32,2048]{1,0:T(8,128)(2,1)} %get-tuple-element.169) | copy-start | bytes 393220 | tf_op jit(solution)/shard_map/cond
  2.1 9.8 %copy-start.2 = (f32[1,2048]{1,0:T(1,128)S(1)}, f32[1,2048]{1,0:T(1,128)}, u32[]{:S(2)}) copy-start(f32[1,2048]{1,0:T(1,128)} %get-tuple-element.171) | copy-start | bytes 24580 | tf_op jit(solution)/shard_map/cond
  3.3 8.6 %slice-start.7 = ((s8[8388608]{0:T(1024)(128)(4,1)}), s8[4194304]{0:T(1024)(128)(4,1)S(1)}, s32[]{:S(2)}) async-start(s8[8388608]{0:T(1024)(128)(4,1)} %bitcast.176), calls=%async_computation.9 | async-start | bytes 8388608 | tf_op jit(solution)/shard_map/cond
  11.7 22.0 %copy-start.4 = (f32[1,2048]{1,0:T(1,128)S(1)}, f32[1,2048]{1,0:T(1,128)}, u32[]{:S(2)}) copy-start(f32[1,2048]{1,0:T(1,128)} %get-tuple-element.177) | copy-start | bytes 24580 | tf_op jit(solution)/shard_map/cond
  11.7 22.1 %slice-start = ((s8[23068672]{0:T(1024)(128)(4,1)}), s8[4194304]{0:T(1024)(128)(4,1)S(1)}, s32[]{:S(2)}) async-start(s8[23068672]{0:T(1024)(128)(4,1)} %bitcast.174), calls=%async_computation.2 | async-start | bytes 8388608 | tf_op jit(solution)/shard_map/cond
  12.0 21.8 %slice-start.1 = ((s8[23068672]{0:T(1024)(128)(4,1)}), s8[4194304]{0:T(1024)(128)(4,1)S(1)}, s32[]{:S(2)}) async-start(s8[23068672]{0:T(1024)(128)(4,1)} %bitcast.174), calls=%async_computation.3 | async-start | bytes 8388608 | tf_op jit(solution)/shard_map/cond
  12.0 21.8 %slice-start.2 = ((s8[23068672]{0:T(1024)(128)(4,1)}), s8[4194304]{0:T(1024)(128)(4,1)S(1)}, s32[]{:S(2)}) async-start(s8[23068672]{0:T(1024)(128)(4,1)} %bitcast.174), calls=%async_computation.4 | async-start | bytes 8388608 | tf_op jit(solution)/shard_map/cond
  13.5 20.2 %slice-start.3 = ((s8[23068672]{0:T(1024)(128)(4,1)}), s8[4194304]{0:T(1024)(128)(4,1)S(1)}, s32[]{:S(2)}) async-start(s8[23068672]{0:T(1024)(128)(4,1)} %bitcast.174), calls=%async_computation.5 | async-start | bytes 8388608 | tf_op jit(solution)/shard_map/cond
  22.8 10.9 %slice-start.4 = ((s8[23068672]{0:T(1024)(128)(4,1)}), s8[4194304]{0:T(1024)(128)(4,1)S(1)}, s32[]{:S(2)}) async-start(s8[23068672]{0:T(1024)(128)(4,1)} %bitcast.174), calls=%async_computation.6 | async-start | bytes 8388608 | tf_op jit(solution)/shard_map/cond
  28.8 5.0 %slice-start.5 = ((s8[23068672]{0:T(1024)(128)(4,1)}), s8[2097152]{0:T(1024)(128)(4,1)S(1)}, s32[]{:S(2)}) async-start(s8[23068672]{0:T(1024)(128)(4,1)} %bitcast.174), calls=%async_computation.7 | async-start | bytes 4194304 | tf_op jit(solution)/shard_map/cond
  77.7 11.0 %collective-permute-start = (bf16[4,15,2,2048]{3,2,1,0:T(2,128)(2,1)S(1)}, bf16[4,15,2,2048]{3,2,1,0:T(2,128)(2,1)S(1)}, u32[]{:S(2)}, u32[]{:S(2)}) collective-permute-start(bf16[4,15,2,2048]{3,2,1,0:T(2,128)(2,1)S(1)} %all_to_all.10), channel_id=1, source_target_pairs={{0,2},{1,3},{4,6},{5,7},{8,10},{9,11},{12,14},{13,15},{16,18},{17,... | collective-permute-start | bytes 1474568 | tf_op jit(solution)/shard_map/ppermute | solution.py:149
  88.7 103.4 %copy-start.3 = (s32[1,32,4]{1,2,0:T(4,128)S(1)}, s32[1,32,4]{1,2,0:T(4,128)}, u32[]{:S(2)}) copy-start(s32[1,32,4]{1,2,0:T(4,128)} %param.25) | copy-start | bytes 1540
  89.4 98.6 %collective-permute-start.1 = (bf16[4,15,2,2048]{3,2,1,0:T(2,128)(2,1)S(1)}, bf16[4,15,2,2048]{3,2,1,0:T(2,128)(2,1)}, u32[]{:S(2)}, u32[]{:S(2)}) collective-permute-start(bf16[4,15,2,2048]{3,2,1,0:T(2,128)(2,1)S(1)} %copy.81), channel_id=1, source_target_pairs={{2,0},{3,1},{6,4},{7,5},{10,8},{11,9},{14,12},{15,13},{18,16},{19,... | collective-permute-start | bytes 1474568 | tf_op jit(solution)/shard_map/ppermute | solution.py:151
  188.0 15.7 %all-to-all-start.1 = ((bf16[4,15,2,2048]{3,2,1,0:T(2,128)(2,1)}), bf16[4,15,2,2048]{3,2,1,0:T(2,128)(2,1)S(1)}, u32[]{:S(2)}, u32[]{:S(2)}) async-start(bf16[4,15,2,2048]{3,2,1,0:T(2,128)(2,1)} %collective-permute-done.1), calls=%async_computation.1 | async-start | bytes 983040 | tf_op jit(solution)/shard_map/all_to_all | solution.py:152
where the time goes:
time: 212 us
  waiting for transfers between devices  118 us (56%)
  matrix products  49.8 us (23%)
  blocking collectives  25.7 us (12%)
  local copies, waits for them, and re-layouts  6.92 us (3%)
  starting transfers between devices  6.43 us (3%)
  other arithmetic  4.44 us (2%)
    ppermute x1, waiting for transfers between devices, device_fn(): back_buf = lax.ppermute(expert_res, 'side', to_attn)  97.3 us
    all_to_all x1, blocking collectives, device_fn(): lax.all_to_all(send_buf.reshape(num_dev, local_experts, capacity, model_d...  19.9 us
    dot_general x1, matrix products, dense_swiglu(): jnp.dot(inner_act, down_w, preferred_element_type=jnp.float32)  17.5 us
    all_to_all x1, waiting for transfers between devices, device_fn(): lax.all_to_all(back_buf, 'dev', 0, 0)  10.9 us
    ppermute x1, waiting for transfers between devices, device_fn(): arrived = lax.ppermute(spread, 'side', to_expert)  9.68 us
    dot_general x1, matrix products, attend(): jnp.einsum('tkgd,tksd->tkgs', q_rows, key_cache, preferred_element_type=j...  8.55 us
    dot_general x1, matrix products, attend(): jnp.dot(in_rows, w_keyval, preferred_element_type=jnp.float32)  8.32 us
    dot_general x1, matrix products, attend(): jnp.einsum('tkgs,tksd->tkgd', prob_bf, val_cache, preferred_element_type=...  5.8 us
  transfers between devices with their start and end apart: 3, of which 3 were waited for; matrix products, arithmetic and copies ran while one was open for 0% of the time, Pallas kernels for 0%

commit v1 on v0

v1 whole, which is shorter than its diff:
```python
import functools
import math

import jax
import jax.numpy as jnp
from jax import lax
from jax.experimental import pallas as pl
from jax.experimental.pallas import tpu as pltpu
from jax.sharding import PartitionSpec as P

NORM_EPS = 1e-6
ROPE_BASE = 10000.0
MESH = pl.DeviceIdType.MESH
BF = jnp.bfloat16
F32 = jnp.float32

ROWS = 32
COLS = 512
HEADS = 4
DIM = 2048
FF = 1408
NA = 4
NB = 3


def rms(rows_f, gain):
    inv = lax.rsqrt(jnp.mean(rows_f * rows_f, axis=-1, keepdims=True) + NORM_EPS)
    return (rows_f * inv * gain).astype(BF)


def iota(shape, axis):
    return lax.broadcasted_iota(jnp.int32, shape, axis)


def silu(v):
    return v * jax.nn.sigmoid(v)


def kernel(hid, kc, vc, lens, ids, gts, ga, gf, wq, wkv, wo, sg, su, sd, wg, wu, wd, out,
           hidv, hidc, lensv, idsv, gtsv, gav, gfv, wqkv, wob, kb, vb, abuf, bbuf,
           idsx, cbuf, mbuf, ubuf, xbuf, hbuf, ybuf, rbuf, spart, srecv, obuf,
           sm, wsem, asem, bsem, isend, irecv, csend, crecv, zsend, zrecv, ysend, yrecv, dsend, drecv,
           esend, erecv, rsend, rrecv, ssend, srec, osend, orecv, olocal):
    d = lax.axis_index("dev")
    s = lax.axis_index("side")
    col = pl.ds(pl.multiple_of(s * COLS, COLS), COLS)
    last = s == 3

    small = [(hid, hidv), (hid.at[:, col], hidc), (lens, lensv), (ids.at[0], idsv), (gts.at[0], gtsv), (ga, gav), (gf, gfv)]
    small = [pltpu.make_async_copy(a, b, sm.at[n]) for n, (a, b) in enumerate(small)]
    for c in small:
        c.start()
    vcol = pl.ds(pl.multiple_of(DIM + s * COLS, COLS), COLS)
    big = [(wq.at[0, :, col], wqkv.at[0]), (wkv.at[0, :, col], wqkv.at[1]), (wkv.at[0, :, vcol], wqkv.at[2]),
           (kc.at[0, :, pl.ds(s * HEADS, HEADS)], kb), (vc.at[0, :, pl.ds(s * HEADS, HEADS)], vb), (wo.at[0, :, col], wob)]
    big = [pltpu.make_async_copy(a, b, wsem.at[n]) for n, (a, b) in enumerate(big)]
    for c in big:
        c.start()

    barrier = pltpu.get_barrier_semaphore()
    for k in range(1, 16):
        peer = {"dev": (d + k // 4) % 4, "side": (s + k % 4) % 4}
        pl.semaphore_signal(barrier, inc=1, device_id=peer, device_id_type=MESH)

    ffcol = pl.ds(pl.multiple_of(d * FF, 128), FF)
    shift = jnp.where(last, 1, 0)

    def local_expert(p):
        return 4 * s + p - shift

    def a_copy(p, which, slot):
        src = (wg, wu)[which]
        return pltpu.make_async_copy(src.at[0, local_expert(p)], abuf.at[slot], asem.at[slot])

    def b_copy(p, slot):
        return pltpu.make_async_copy(wd.at[0, local_expert(p)], bbuf.at[slot], bsem.at[slot])

    def first_unit_starts():
        @pl.when(last)
        def _():
            pltpu.make_async_copy(sg.at[0, :, ffcol], abuf.at[0], asem.at[0]).start()
            pltpu.make_async_copy(su.at[0, :, ffcol], abuf.at[1], asem.at[1]).start()
            pltpu.make_async_copy(sd.at[0, pl.ds(pl.multiple_of(d * FF, 128), FF)], bbuf.at[0], bsem.at[0]).start()

        @pl.when(jnp.logical_not(last))
        def _():
            a_copy(0, 0, 0).start()
            a_copy(0, 1, 1).start()
            b_copy(0, 0).start()

    for c in small:
        c.wait()
    normed = rms(hidv[...].astype(F32), gav[...])
    lens_row = lensv[...].astype(F32)
    eye = iota((ROWS, ROWS), 0) == iota((ROWS, ROWS), 1)
    lens_col = jnp.sum(jnp.where(eye, jnp.broadcast_to(lens_row, (ROWS, ROWS)), 0.0), axis=1, keepdims=True)
    lane = iota((ROWS, 128), 1)
    freq = jnp.exp((lane & 63).astype(F32) * (-2.0 * math.log(ROPE_BASE) / 128.0))
    angle = lens_col * freq
    cosine = jnp.cos(angle)
    sine = jnp.where(lane < 64, -jnp.sin(angle), jnp.sin(angle))

    def rope(v):
        return (v * cosine + pltpu.roll(v, 64, axis=1) * sine).astype(BF).astype(F32)

    idf = idsv[...].astype(F32)
    lane32 = iota((ROWS, 128), 1) == d * ROWS + iota((ROWS, 128), 0)
    for j in range(4):
        idsx[d, j:j + 1, :] = jnp.sum(jnp.where(lane32, jnp.broadcast_to(idf[:, j:j + 1], (ROWS, 128)), 0.0), axis=0, keepdims=True)
    for j in range(4):
        rbuf[j, 3, 0] = jnp.zeros((8, 256), BF)

    big[0].wait()
    big[1].wait()
    big[2].wait()
    first_unit_starts()
    a_copy(1, 0, 2).start()
    a_copy(1, 1, 3).start()
    b_copy(1, 1).start()
    b_copy(2, 2).start()
    q_all = jnp.dot(normed, wqkv[0], preferred_element_type=F32).astype(BF).astype(F32)
    k_all = jnp.dot(normed, wqkv[1], preferred_element_type=F32).astype(BF).astype(F32)
    v_all = jnp.dot(normed, wqkv[2], preferred_element_type=F32).astype(BF).astype(F32)
    q_h = [rope(q_all[:, 128 * h:128 * h + 128]) for h in range(HEADS)]
    k_h = [rope(k_all[:, 128 * h:128 * h + 128]) for h in range(HEADS)]
    v_h = [v_all[:, 128 * h:128 * h + 128] for h in range(HEADS)]

    row8 = iota((8, 128), 0)
    big[3].wait()
    parts = []
    for h in range(HEADS):
        for g in range(4):
            q8 = q_h[h][8 * g:8 * g + 8].astype(BF)
            keys = kb[8 * g:8 * g + 8, h].reshape(8 * 128, 128)
            full = lax.dot_general(q8, keys, (((1,), (1,)), ((), ())), preferred_element_type=F32)
            acc = jnp.zeros((8, 128), F32)
            for t in range(8):
                acc = acc + jnp.where(row8 == t, full[:, 128 * t:128 * t + 128], 0.0)
            parts.append(acc)
    scale = 128 ** -0.5
    scores = jnp.concatenate(parts, axis=0) * scale
    q_cat = jnp.concatenate(q_h, axis=0)
    k_cat = jnp.concatenate(k_h, axis=0)
    v_cat = jnp.concatenate(v_h, axis=0)
    lens_cat = jnp.concatenate([lens_col] * HEADS, axis=0)
    scores = jnp.where(iota((128, 128), 1).astype(F32) < lens_cat, scores, -jnp.inf)
    self_score = jnp.sum(q_cat * k_cat, axis=1, keepdims=True) * scale
    peak = jnp.maximum(jnp.max(scores, axis=1, keepdims=True), self_score)
    weights = jnp.exp(scores - peak)
    self_weight = jnp.exp(self_score - peak)
    denom = jnp.sum(weights, axis=1, keepdims=True) + self_weight
    prob = (weights / denom).astype(BF).astype(F32)
    self_prob = (self_weight / denom).astype(BF).astype(F32)
    big[4].wait()
    for h in range(HEADS):
        ctx = []
        for g in range(4):
            n = 4 * h + g
            p8 = prob[8 * n:8 * n + 8]
            wide = jnp.concatenate([jnp.where(row8 == t, p8, 0.0) for t in range(8)], axis=1).astype(BF)
            vals = vb[8 * g:8 * g + 8, h].reshape(8 * 128, 128)
            ctx.append(jnp.dot(wide, vals, preferred_element_type=F32))
        ctx = jnp.concatenate(ctx, axis=0)
        ctx = ctx + self_prob[32 * h:32 * h + 32] * v_cat[32 * h:32 * h + 32]
        cbuf[s, :, 128 * h:128 * h + 128] = ctx.astype(BF)

    pl.semaphore_wait(barrier, 15)
    ccopies = []
    for k in range(1, 4):
        c = pltpu.make_async_remote_copy(cbuf.at[s], cbuf.at[s], csend.at[k], crecv.at[k],
                                         device_id={"side": (s + k) % 4}, device_id_type=MESH)
        c.start()
        ccopies.append(c)
    icopies = []
    for k in range(1, 4):
        c = pltpu.make_async_remote_copy(idsx.at[d], idsx.at[d], isend.at[k], irecv.at[k],
                                         device_id={"dev": (d + k) % 4}, device_id_type=MESH)
        c.start()
        icopies.append(c)
    big[5].wait()
    for c in ccopies:
        c.wait_recv()
    mid = hidc[...].astype(F32)
    attn = jnp.zeros((ROWS, COLS), F32)
    for n in range(4):
        attn = attn + jnp.dot(cbuf[n], wob[COLS * n:COLS * n + COLS], preferred_element_type=F32)
    mid = (mid + attn).astype(BF)
    mbuf[d, s] = mid

    dx = (d, d + 1 - 2 * (d % 2), (d + 2) % 4, 3 - d)
    sx = (s, s + 1 - 2 * (s % 2), (s + 2) % 4, 3 - s)

    def tile_copy(tile, send, recv, peer):
        return pltpu.make_async_remote_copy(tile, tile, send, recv, device_id=peer, device_id_type=MESH)

    zc = [None] + [tile_copy(mbuf.at[d, s], zsend.at[k], zrecv.at[k], {"dev": dx[k]}) for k in range(1, 4)]
    yc = [tile_copy(mbuf.at[dx[q], s], ysend.at[q], yrecv.at[q], {"side": sx[2]}) for q in range(4)]
    dc = [tile_copy(mbuf.at[dx[q], s], dsend.at[q], drecv.at[q], {"side": sx[1]}) for q in range(4)]
    ec = [tile_copy(mbuf.at[dx[q], sx[2]], esend.at[q], erecv.at[q], {"side": sx[1]}) for q in range(4)]
    for k in range(1, 4):
        zc[k].start()
    yc[0].start()
    dc[0].start()

    for c in icopies:
        c.wait_recv()
    id_all = idsx[0] + idsx[1] + idsx[2] + idsx[3]
    r = iota((128, 128), 0)
    t = iota((128, 128), 1)
    unit = r >> 5
    expert = d * 15 + local_expert(unit)
    expert = jnp.where(jnp.logical_and(last, unit == 0), -1, expert).astype(F32)
    hit = jnp.zeros((128, 128), F32)
    for j in range(4):
        hit = hit + jnp.where(jnp.broadcast_to(id_all[j:j + 1], (128, 128)) == expert, 1.0, 0.0)
    earlier = jnp.where(jnp.logical_and(r >> 4 == t >> 4, r < t), 1.0, 0.0).astype(BF)
    rank = jnp.dot(hit.astype(BF), earlier, preferred_element_type=F32)
    place = jnp.logical_and(rank == (r & 1).astype(F32), t >> 4 == 2 * ((r >> 3) & 3) + ((r >> 1) & 1))
    pick = jnp.where(place, hit, 0.0).astype(BF)

    def norm_plane(q):
        dc[q].wait_recv()
        ec[q].wait_recv()
        rows = jnp.concatenate([mbuf[dx[q], n] for n in range(4)], axis=1).astype(F32)
        ubuf[pl.ds(pl.multiple_of(dx[q] * ROWS, ROWS), ROWS), :] = rms(rows, gfv[...])

    yc[0].wait_recv()
    ec[0].start()
    zc[1].wait_recv()
    yc[1].start()
    dc[1].start()
    yc[1].wait_recv()
    ec[1].start()
    zc[2].wait_recv()
    yc[2].start()
    dc[2].start()
    zc[3].wait_recv()
    yc[3].start()
    dc[3].start()
    yc[2].wait_recv()
    ec[2].start()
    yc[3].wait_recv()
    ec[3].start()
    for q in range(4):
        norm_plane(q)
    for n in range(4):
        xs = jnp.dot(pick, ubuf[:, COLS * n:COLS * n + COLS], preferred_element_type=F32).astype(BF)
        xbuf[:, COLS * n:COLS * n + COLS] = xs

    peers = [((d + k // 4) % 4, (s + k % 4) % 4) for k in range(16)]
    low = (iota((32, 256), 0) & 7) < 4
    chunks = [(256 * n, 256) for n in range(5)] + [(1280, 128)]

    def ring_copy(p, k):
        pd, ps = peers[k]
        return pltpu.make_async_remote_copy(ybuf.at[p, pd, ps], rbuf.at[d, s, p], rsend.at[p, k], rrecv.at[p, k],
                                            device_id={"dev": pd, "side": ps}, device_id_type=MESH)

    def part_copy(k):
        pd, ps = peers[k]
        return pltpu.make_async_remote_copy(spart.at[pd, ps], srecv.at[d], ssend.at[k], srec.at[k],
                                            device_id={"dev": pd, "side": ps}, device_id_type=MESH)

    def inner(rows, slot0, slot1, m):
        for off, width in chunks:
            gate = jnp.dot(rows, abuf[slot0, :, off:off + width], preferred_element_type=F32)
            up = jnp.dot(rows, abuf[slot1, :, off:off + width], preferred_element_type=F32)
            hbuf[0:m, off:off + width] = (silu(gate) * up).astype(BF)

    def unit_body(p, carry):
        slot0 = (2 * p) % NA
        slot1 = (2 * p + 1) % NA
        slotb = p % NB
        pltpu.make_async_copy(wg.at[0, 0], abuf.at[slot0], asem.at[slot0]).wait()
        pltpu.make_async_copy(wu.at[0, 0], abuf.at[slot1], asem.at[slot1]).wait()
        is_shared = jnp.logical_and(last, p == 0)

        @pl.when(is_shared)
        def _():
            inner(ubuf[...], slot0, slot1, 128)

        @pl.when(jnp.logical_not(is_shared))
        def _():
            inner(xbuf[pl.ds(pl.multiple_of(p * 32, 32), 32), :], slot0, slot1, 32)

        @pl.when(p < 2)
        def _():
            a_copy(p + 2, 0, slot0).start()
            a_copy(p + 2, 1, slot1).start()

        pltpu.make_async_copy(wd.at[0, 0], bbuf.at[slotb], bsem.at[slotb]).wait()

        @pl.when(is_shared)
        def _():
            rows = hbuf[...]
            for n in range(4):
                for half in range(2):
                    off = COLS * n + 256 * half
                    res = jnp.dot(rows, bbuf[slotb, :, off:off + 256], preferred_element_type=F32)
                    for pd in range(4):
                        spart[pd, n, :, 256 * half:256 * half + 256] = res[32 * pd:32 * pd + 32]
            for k in range(1, 16):
                part_copy(k).start()
            srecv[d] = spart[d, 3]

        @pl.when(jnp.logical_not(is_shared))
        def _():
            rows = hbuf[0:32, :]
            for n in range(4):
                left = jnp.dot(rows, bbuf[slotb, :, COLS * n:COLS * n + 256], preferred_element_type=F32)
                right = jnp.dot(rows, bbuf[slotb, :, COLS * n + 256:COLS * n + 512], preferred_element_type=F32)
                packed = jnp.where(low, left, right)
                for pd in range(4):
                    ybuf[p, pd, n] = packed[8 * pd:8 * pd + 8].astype(BF)
            for k in range(1, 16):
                ring_copy(p, k).start()
            rbuf[d, s, p] = ybuf[p, d, s]

        @pl.when(p < 1)
        def _():
            b_copy(p + 3, slotb).start()

        return carry

    lax.fori_loop(0, 4, unit_body, 0)

    lanes = 512
    l = iota((ROWS, lanes), 1)
    tok = iota((ROWS, lanes), 0)
    lside = (l >> 5) & 3
    lunit = (l >> 3) & 3
    lexp = 15 * (l >> 7) + 4 * lside + lunit - jnp.where(lside == 3, 1, 0)
    lexp = jnp.where(jnp.logical_and(lside == 3, lunit == 0), -1, lexp).astype(F32)
    hits = jnp.zeros((ROWS, lanes), F32)
    gated = jnp.zeros((ROWS, lanes), F32)
    gates = gtsv[...]
    for j in range(4):
        same = jnp.broadcast_to(idf[:, j:j + 1], (ROWS, lanes)) == lexp
        hits = hits + jnp.where(same, 1.0, 0.0)
        gated = gated + jnp.where(same, jnp.broadcast_to(gates[:, j:j + 1], (ROWS, lanes)), 0.0)
    a0 = iota((ROWS, ROWS), 0)
    a1 = iota((ROWS, ROWS), 1)
    before = jnp.where(jnp.logical_and(a0 >> 4 == a1 >> 4, a1 < a0), 1.0, 0.0).astype(BF)
    order = jnp.dot(before, hits.astype(BF), preferred_element_type=F32)
    fits = jnp.logical_and(order == (l & 1).astype(F32), (tok >> 4) == ((l >> 1) & 1))
    gated = jnp.where(fits, gated, 0.0)
    stack = []
    for half in range(2):
        g = jnp.where(((l >> 2) & 1) == half, gated, 0.0)
        for _ in range(3):
            piece = g.astype(BF)
            stack.append(piece)
            g = g - piece.astype(F32)
    stack = jnp.concatenate(stack, axis=0)

    for p in range(4):
        for k in range(1, 16):
            if p == 0:
                from_last = peers_side_is_last(s, k)

                @pl.when(jnp.logical_not(from_last))
                def _():
                    ring_copy(p, k).wait_recv()

                @pl.when(from_last)
                def _():
                    part_copy(k).wait_recv()
            else:
                ring_copy(p, k).wait_recv()
    got = jnp.dot(stack, rbuf[...].reshape(512, 256), preferred_element_type=F32)
    routed = jnp.concatenate([got[0:32] + got[32:64] + got[64:96], got[96:128] + got[128:160] + got[160:192]], axis=1)
    shared = (srecv[0] + srecv[1] + srecv[2] + srecv[3]).astype(BF).astype(F32)
    obuf[...] = (mid.astype(F32) + shared + routed).astype(BF)
    ocopies = [pltpu.make_async_remote_copy(obuf, out.at[:, col], osend.at[k], orecv.at[k],
                                            device_id={"side": (s + k) % 4}, device_id_type=MESH) for k in range(1, 4)]
    for c in ocopies:
        c.start()
    mine = pltpu.make_async_copy(obuf, out.at[:, col], olocal)
    mine.start()

    for c in ccopies + icopies + zc[1:] + yc + dc + ec:
        c.wait_send()

    @pl.when(last)
    def _():
        for k in range(1, 16):
            part_copy(k).wait_send()

    @pl.when(jnp.logical_not(last))
    def _():
        for k in range(1, 16):
            ring_copy(0, k).wait_send()

    for p in range(1, 4):
        for k in range(1, 16):
            ring_copy(p, k).wait_send()
    mine.wait()
    for c in ocopies:
        c.wait()


def peers_side_is_last(s, k):
    return (s + 4 - k % 4) % 4 == 3


def solution(mesh):
    def device_fn(hidden, k_cache, v_cache, cache_lens, expert_ids, route_gates, *weights):
        any_spec = pl.BlockSpec(memory_space=pl.ANY)
        dma = pltpu.SemaphoreType.DMA
        vm = pltpu.VMEM
        return pl.pallas_call(
            kernel,
            out_shape=jax.ShapeDtypeStruct((ROWS, DIM), BF),
            in_specs=[any_spec] * 17,
            out_specs=any_spec,
            scratch_shapes=[
                vm((ROWS, DIM), BF), vm((ROWS, COLS), BF), vm((1, ROWS), jnp.int32), vm((ROWS, 4), jnp.int32),
                vm((ROWS, 4), F32), vm((1, DIM), F32), vm((1, DIM), F32),
                vm((3, DIM, COLS), BF), vm((DIM, COLS), BF),
                vm((ROWS, HEADS, 128, 128), BF), vm((ROWS, HEADS, 128, 128), BF),
                vm((NA, DIM, FF), BF), vm((NB, FF, DIM), BF),
                vm((4, 8, 128), F32), vm((4, ROWS, COLS), BF), vm((4, 4, ROWS, COLS), BF),
                vm((128, DIM), BF), vm((128, DIM), BF), vm((128, FF), BF),
                vm((4, 4, 4, 8, 256), BF), vm((4, 4, 4, 8, 256), BF),
                vm((4, 4, ROWS, COLS), F32), vm((4, ROWS, COLS), F32), vm((ROWS, COLS), BF),
                dma((7,)), dma((6,)), dma((NA,)), dma((NB,)), dma((4,)), dma((4,)), dma((4,)), dma((4,)),
                dma((4,)), dma((4,)), dma((4,)), dma((4,)), dma((4,)), dma((4,)), dma((4,)), dma((4,)),
                dma((4, 16)), dma((4, 16)), dma((16,)), dma((16,)), dma((4,)), dma((4,)), dma,
            ],
            compiler_params=pltpu.CompilerParams(collective_id=0, has_side_effects=True, vmem_limit_bytes=67000000),
            name="moe_decode",
        )(hidden, k_cache, v_cache, cache_lens.reshape(1, ROWS), expert_ids, route_gates, *weights)

    batch = P(("inst", "dev"))
    layer = P(None, ("inst", "dev"))
    expert = P(None, "dev")
    in_specs = (batch, layer, layer, batch, layer, layer) + (P(),) * 8 + (expert,) * 3
    return jax.shard_map(device_fn, mesh=mesh, in_specs=in_specs, out_specs=batch, check_vma=False)
```

time: 212 us -> 57.3 us (0.27)
  waiting for transfers between devices: 118 us -> 0 us
  Pallas kernels: 0 us -> 52.9 us
  matrix products: 49.8 us -> 0 us
  blocking collectives: 25.7 us -> 0 us
  starting transfers between devices: 6.43 us -> 0 us
  other arithmetic: 4.44 us -> 0 us
  local copies, waits for them, and re-layouts: 6.92 us -> 4.29 us
    ppermute x2 -> x0, waiting for transfers between devices: 107 us -> none  [the longest x1 97.3 us: device_fn(): back_buf = lax.ppermute(expert_res, 'side', to_attn)]
    pallas_call x0 -> x1, Pallas kernels: none -> 52.9 us  [device_fn(): pl.pallas_call(kernel, out_shape=jax.ShapeDtypeStruct((ROWS, DIM), BF), i...]
    dot_general x9 -> x0, matrix products: 49.8 us -> none  [the longest x1 17.5 us: dense_swiglu(): jnp.dot(inner_act, down_w, preferred_element_type=jnp.float32)]
    all_to_all x1 -> x0, blocking collectives: 19.9 us -> none  [device_fn(): lax.all_to_all(send_buf.reshape(num_dev, local_experts, capacity, model_d...]
    all_to_all x1 -> x0, waiting for transfers between devices: 10.9 us -> none  [device_fn(): lax.all_to_all(back_buf, 'dev', 0, 0)]
    all_gather x1 -> x0, blocking collectives: 5.78 us -> none  [device_fn(): gathered = lax.all_gather(x_state, 'side')]
    unnamed x4 -> x3, local copies, waits for them, and re-layouts: 0.01 us -> 4.29 us
    all_to_all x1 -> x0, starting transfers between devices: 3.83 us -> none  [device_fn(): lax.all_to_all(back_buf, 'dev', 0, 0)]
  transfers between devices with their start and end apart: 3 -> 0, of which waited for: 3 -> 0; matrix products, arithmetic and copies ran while one was open for 0% -> 0% of each run, Pallas kernels for 0% -> 0%
where the time goes in v1:
time: 57.3 us; the launch traced here: 57.2 us
  Pallas kernels  52.9 us (92%)
  local copies, waits for them, and re-layouts  4.29 us (7%)
    pallas_call x1, Pallas kernels, device_fn(): pl.pallas_call(kernel, out_shape=jax.ShapeDtypeStruct((ROWS, DIM), BF), i...  52.9 us
    unnamed x3, local copies, waits for them, and re-layouts  4.29 us

profile of v1, /device:TPU:0, one launch (start us, length us, event | category | flops | bytes accessed | tf_op | source)
XLA Modules:
  0.0 57.2 jit_solution(8343127524467557517)
XLA Ops:
  0.0 1.4 %copy.18.ids = s32[1,32,4]{2,1,0:T(8,128)} copy(s32[1,32,4]{1,2,0:T(4,128)} %param.21) | data formatting | bytes 1024 | tf_op args[4]
  1.4 1.4 %copy.19.gts = f32[1,32,4]{2,1,0:T(8,128)} copy(f32[1,32,4]{1,2,0:T(4,128)} %param.22) | data formatting | bytes 1024 | tf_op args[5]
  2.7 52.9 %moe_decode.1 = bf16[32,2048]{1,0:T(8,128)(2,1)} custom-call(bf16[32,2048]{1,0:T(8,128)(2,1)} %hid.1, bf16[1,32,16,128,128]{4,3,2,1,0:T(8,128)(2,1)} %kc.1, bf16[1,32,16,128,128]{4,3,2,1,0:T(8,128)(2,1)} %vc.1, s32[1,32]{1,0:T(1,128)} %bitcast.1, s32[1,32,4]{2,1,0:T(8,128)} %copy.18.ids, f32[1,32,4]{2,1,0:T(8,128)} %copy.19.gts, f32[1,2048]{1,0:T(1,128)} %ga.1, ...), custom_call_target="tpu_custom_call" | custom-call | tf_op jit(solution)/shard_map/moe_decode/pallas_call | solution.py:411
  55.6 1.6 %copy.21 = bf16[32,2048]{1,0:T(8,128)(2,1)} copy(bf16[32,2048]{1,0:T(8,128)(2,1)} %moe_decode.1) | data formatting | bytes 262144

commit v2 on v1

v2 whole, which is shorter than its diff:
```python
import functools
import math

import jax
import jax.numpy as jnp
from jax import lax
from jax.experimental import pallas as pl
from jax.experimental.pallas import tpu as pltpu
from jax.sharding import PartitionSpec as P

NORM_EPS = 1e-6
ROPE_BASE = 10000.0
MESH = pl.DeviceIdType.MESH
BF = jnp.bfloat16
F32 = jnp.float32

ROWS = 32
COLS = 512
HEADS = 4
DIM = 2048
FF = 1408
NA = 5
NB = 4


def rms(rows_f, gain):
    inv = lax.rsqrt(jnp.mean(rows_f * rows_f, axis=-1, keepdims=True) + NORM_EPS)
    return (rows_f * inv * gain).astype(BF)


def iota(shape, axis):
    return lax.broadcasted_iota(jnp.int32, shape, axis)


def silu(v):
    return v * jax.nn.sigmoid(v)


def kernel(hid, kc, vc, lens, ids, gts, ga, gf, wq, wkv, wo, sg, su, sd, wg, wu, wd, out,
           hidv, hidc, lensv, idsv, gtsv, gav, gfv, kb, vb, abuf, bbuf,
           idsx, cbuf, mbuf, ubuf, xbuf, hbuf, ybuf, rbuf, spart, srecv, obuf, stackv,
           sm, wsem, asem, bsem, isend, irecv, csend, crecv, msend, zrecv, yrecv, drecv, erecv,
           rsend, rrecv, ssend, srec, osend, orecv, olocal):
    d = lax.axis_index("dev")
    s = lax.axis_index("side")
    col = pl.ds(pl.multiple_of(s * COLS, COLS), COLS)

    small = [(hid, hidv), (hid.at[:, col], hidc), (lens, lensv), (ids.at[0], idsv), (gts.at[0], gtsv), (ga, gav), (gf, gfv)]
    small = [pltpu.make_async_copy(a, b, sm.at[n]) for n, (a, b) in enumerate(small)]
    for c in small:
        c.start()
    vcol = pl.ds(pl.multiple_of(DIM + s * COLS, COLS), COLS)
    wqv, wkv_k, wkv_v, wob = abuf.at[3, :, 0:512], abuf.at[3, :, 512:1024], abuf.at[4, :, 0:512], abuf.at[4, :, 512:1024]
    big = [(wq.at[0, :, col], wqv), (wkv.at[0, :, col], wkv_k), (wkv.at[0, :, vcol], wkv_v),
           (kc.at[0, :, pl.ds(s * HEADS, HEADS)], kb), (vc.at[0, :, pl.ds(s * HEADS, HEADS)], vb), (wo.at[0, :, col], wob)]
    big = [pltpu.make_async_copy(a, b, wsem.at[n]) for n, (a, b) in enumerate(big)]
    for n in range(3):
        big[n].start()

    barrier = pltpu.get_barrier_semaphore()
    for k in range(1, 16):
        peer = {"dev": (d + k // 4) % 4, "side": (s + k % 4) % 4}
        pl.semaphore_signal(barrier, inc=1, device_id=peer, device_id_type=MESH)

    ffcol = pl.ds(pl.multiple_of(s * FF, 128), FF)

    def local_expert(p):
        return jnp.minimum(4 * s + p, 14)

    def a_copy(n):
        slot = n % NA
        if n < 2:
            return pltpu.make_async_copy((sg, su)[n].at[0, :, ffcol], abuf.at[slot], asem.at[slot])
        return pltpu.make_async_copy((wg, wu)[n % 2].at[0, local_expert(n // 2 - 1)], abuf.at[slot], asem.at[slot])

    def b_copy(n):
        slot = n % NB
        src = sd.at[0, ffcol] if n == 0 else wd.at[0, local_expert(n - 1)]
        return pltpu.make_async_copy(src, bbuf.at[slot], bsem.at[slot])

    for c in small:
        c.wait()
    big[3].start()
    normed = rms(hidv[...].astype(F32), gav[...])
    lens_row = lensv[...].astype(F32)
    eye = iota((ROWS, ROWS), 0) == iota((ROWS, ROWS), 1)
    lens_col = jnp.sum(jnp.where(eye, jnp.broadcast_to(lens_row, (ROWS, ROWS)), 0.0), axis=1, keepdims=True)
    lane = iota((ROWS, 128), 1)
    freq = jnp.exp((lane & 63).astype(F32) * (-2.0 * math.log(ROPE_BASE) / 128.0))
    angle = lens_col * freq
    cosine = jnp.cos(angle)
    sine = jnp.where(lane < 64, -jnp.sin(angle), jnp.sin(angle))

    def rope(v):
        return (v * cosine + pltpu.roll(v, 64, axis=1) * sine).astype(BF).astype(F32)

    idf = idsv[...].astype(F32)
    wide_ids = jnp.concatenate([idf] * 4, axis=1)
    idsx[d, 0:4, :] = jnp.where(iota((4, 128), 1) >> 5 == d, wide_ids, 0.0)
    idsx[d, 4:8, :] = jnp.zeros((4, 128), F32)

    big[0].wait()
    big[4].start()
    q_all = jnp.dot(normed, wqv[...], preferred_element_type=F32).astype(BF).astype(F32)
    big[1].wait()
    big[5].start()
    a_copy(0).start()
    a_copy(1).start()
    b_copy(0).start()
    k_all = jnp.dot(normed, wkv_k[...], preferred_element_type=F32).astype(BF).astype(F32)
    big[2].wait()
    v_all = jnp.dot(normed, wkv_v[...], preferred_element_type=F32).astype(BF).astype(F32)
    a_copy(2).start()
    a_copy(3).start()
    b_copy(1).start()
    b_copy(2).start()
    b_copy(3).start()

    q_h = [rope(q_all[:, 128 * h:128 * h + 128]) for h in range(HEADS)]
    k_h = [rope(k_all[:, 128 * h:128 * h + 128]) for h in range(HEADS)]
    v_h = [v_all[:, 128 * h:128 * h + 128] for h in range(HEADS)]

    row8 = iota((8, 128), 0)
    big[3].wait()
    parts = []
    for h in range(HEADS):
        for g in range(4):
            q8 = q_h[h][8 * g:8 * g + 8].astype(BF)
            keys = kb[8 * g:8 * g + 8, h].reshape(8 * 128, 128)
            full = lax.dot_general(q8, keys, (((1,), (1,)), ((), ())), preferred_element_type=F32)
            acc = jnp.zeros((8, 128), F32)
            for t in range(8):
                acc = acc + jnp.where(row8 == t, full[:, 128 * t:128 * t + 128], 0.0)
            parts.append(acc)
    scale = 128 ** -0.5
    scores = jnp.concatenate(parts, axis=0) * scale
    q_cat = jnp.concatenate(q_h, axis=0)
    k_cat = jnp.concatenate(k_h, axis=0)
    v_cat = jnp.concatenate(v_h, axis=0)
    lens_cat = jnp.concatenate([lens_col] * HEADS, axis=0)
    scores = jnp.where(iota((128, 128), 1).astype(F32) < lens_cat, scores, -jnp.inf)
    self_score = jnp.sum(q_cat * k_cat, axis=1, keepdims=True) * scale
    peak = jnp.maximum(jnp.max(scores, axis=1, keepdims=True), self_score)
    weights = jnp.exp(scores - peak)
    self_weight = jnp.exp(self_score - peak)
    denom = jnp.sum(weights, axis=1, keepdims=True) + self_weight
    prob = (weights / denom).astype(BF).astype(F32)
    self_prob = (self_weight / denom).astype(BF).astype(F32)
    big[4].wait()
    for h in range(HEADS):
        ctx = []
        for g in range(4):
            n = 4 * h + g
            p8 = prob[8 * n:8 * n + 8]
            wide = jnp.concatenate([jnp.where(row8 == t, p8, 0.0) for t in range(8)], axis=1).astype(BF)
            vals = vb[8 * g:8 * g + 8, h].reshape(8 * 128, 128)
            ctx.append(jnp.dot(wide, vals, preferred_element_type=F32))
        ctx = jnp.concatenate(ctx, axis=0)
        ctx = ctx + self_prob[32 * h:32 * h + 32] * v_cat[32 * h:32 * h + 32]
        cbuf[s, :, 128 * h:128 * h + 128] = ctx.astype(BF)

    pl.semaphore_wait(barrier, 15)
    ccopies = []
    for k in range(1, 4):
        c = pltpu.make_async_remote_copy(cbuf.at[s], cbuf.at[s], csend, crecv,
                                         device_id={"side": (s + k) % 4}, device_id_type=MESH)
        c.start()
        ccopies.append(c)
    icopies = []
    for k in range(1, 4):
        c = pltpu.make_async_remote_copy(idsx.at[d], idsx.at[d], isend, irecv,
                                         device_id={"dev": (d + k) % 4}, device_id_type=MESH)
        c.start()
        icopies.append(c)

    lanes = 512
    l = iota((ROWS, lanes), 1)
    tok = iota((ROWS, lanes), 0)
    lside = (l >> 5) & 3
    lunit = (l >> 3) & 3
    lexp = 4 * lside + lunit
    lexp = jnp.where(lexp < 15, 15 * (l >> 7) + lexp, -1).astype(F32)
    hits = jnp.zeros((ROWS, lanes), F32)
    gated = jnp.zeros((ROWS, lanes), F32)
    gates = gtsv[...]

    def column(row):
        return jnp.sum(jnp.where(eye, jnp.broadcast_to(row, (ROWS, ROWS)), 0.0), axis=1, keepdims=True)

    for j in range(4):
        same = jnp.broadcast_to(column(idf[j:j + 1]), (ROWS, lanes)) == lexp
        hits = hits + jnp.where(same, 1.0, 0.0)
        gated = gated + jnp.where(same, jnp.broadcast_to(column(gates[j:j + 1]), (ROWS, lanes)), 0.0)
    a0 = iota((ROWS, ROWS), 0)
    a1 = iota((ROWS, ROWS), 1)
    before = jnp.where(jnp.logical_and(a0 >> 4 == a1 >> 4, a1 < a0), 1.0, 0.0).astype(BF)
    order = jnp.dot(before, hits.astype(BF), preferred_element_type=F32)
    fits = jnp.logical_and(order == (l & 1).astype(F32), (tok >> 4) == ((l >> 1) & 1))
    gated = jnp.where(fits, gated, 0.0)
    stack = []
    for half in range(2):
        g = jnp.where(((l >> 2) & 1) == half, gated, 0.0)
        for _ in range(3):
            piece = g.astype(BF)
            stack.append(piece)
            g = g - piece.astype(F32)
    stackv[...] = jnp.concatenate(stack, axis=0)

    big[5].wait()
    pltpu.make_async_copy(cbuf.at[0:3], cbuf.at[0:3], crecv).wait()
    mid = hidc[...].astype(F32)
    attn = jnp.zeros((ROWS, COLS), F32)
    for n in range(4):
        attn = attn + jnp.dot(cbuf[n], wob[COLS * n:COLS * n + COLS, :], preferred_element_type=F32)
    mid = (mid + attn).astype(BF)
    mbuf[4 * d + s] = mid
    a_copy(4).start()

    dx = (d, d + 1 - 2 * (d % 2), (d + 2) % 4, 3 - d)
    sx = (s, s + 1 - 2 * (s % 2), (s + 2) % 4, 3 - s)

    def tile_copy(plane, side, recv, peer):
        tile = mbuf.at[4 * plane + side]
        return pltpu.make_async_remote_copy(tile, tile, msend, recv, device_id=peer, device_id_type=MESH)

    zc = [None] + [tile_copy(d, s, zrecv.at[k - 1], {"dev": dx[k]}) for k in range(1, 4)]
    yc = [tile_copy(dx[q], s, yrecv.at[q], {"side": sx[2]}) for q in range(4)]
    dc = [tile_copy(dx[q], s, drecv.at[q], {"side": sx[1]}) for q in range(4)]
    ec = [tile_copy(dx[q], sx[2], erecv.at[q], {"side": sx[1]}) for q in range(4)]

    def from_z(k):
        zc[k].wait_recv()
        yc[k].start()
        dc[k].start()

    def from_y(q):
        yc[q].wait_recv()
        ec[q].start()

    def norm_plane(q):
        dc[q].wait_recv()
        ec[q].wait_recv()
        rows = jnp.concatenate([mbuf[4 * dx[q] + n] for n in range(4)], axis=1).astype(F32)
        u = rms(rows, gfv[...])
        ubuf[pl.ds(pl.multiple_of(dx[q] * ROWS, ROWS), ROWS), :] = u


    for k in range(1, 4):
        zc[k].start()
    yc[0].start()
    dc[0].start()

    chunks = [(256 * n, 256) for n in range(5)] + [(1280, 128)]

    def inner(rows, slot0, slot1, part):
        for off, width in part:
            gate = jnp.dot(rows, abuf[slot0, :, off:off + width], preferred_element_type=F32)
            up = jnp.dot(rows, abuf[slot1, :, off:off + width], preferred_element_type=F32)
            hbuf[:, off:off + width] = (silu(gate) * up).astype(BF)

    def shared_down(n):
        spart[n] = jnp.dot(hbuf[...], bbuf[0, :, COLS * n:COLS * n + COLS], preferred_element_type=F32)

    from_y(0)
    pltpu.make_async_copy(idsx.at[0:3], idsx.at[0:3], irecv).wait()
    id_all = idsx[0] + idsx[1] + idsx[2] + idsx[3]
    r = iota((128, 128), 0)
    t = iota((128, 128), 1)
    unit = r >> 5
    expert = 4 * s + unit
    expert = jnp.where(expert < 15, d * 15 + expert, -1).astype(F32)
    hit = jnp.zeros((128, 128), F32)
    for j in range(4):
        hit = hit + jnp.where(jnp.broadcast_to(id_all[j:j + 1], (128, 128)) == expert, 1.0, 0.0)
    earlier = jnp.where(jnp.logical_and(r >> 4 == t >> 4, r < t), 1.0, 0.0).astype(BF)
    rank = jnp.dot(hit.astype(BF), earlier, preferred_element_type=F32)
    place = jnp.logical_and(rank == (r & 1).astype(F32), t >> 4 == 2 * ((r >> 3) & 3) + ((r >> 1) & 1))
    pick = jnp.where(place, hit, 0.0).astype(BF)

    from_z(1)
    norm_plane(0)
    mine_rows = pl.ds(pl.multiple_of(d * ROWS, ROWS), ROWS)
    a_copy(0).wait()
    a_copy(1).wait()
    inner(ubuf[mine_rows, :], 0, 1, chunks[0:3])
    from_y(1)
    from_z(2)
    inner(ubuf[mine_rows, :], 0, 1, chunks[3:6])
    a_copy(5).start()
    a_copy(6).start()
    b_copy(0).wait()
    from_z(3)
    shared_down(0)
    shared_down(1)
    from_y(2)
    shared_down(2)
    shared_down(3)
    b_copy(4).start()
    from_y(3)
    for q in range(1, 4):
        norm_plane(q)
    scopies = []
    for k in range(1, 4):
        peer = (s + k) % 4
        c = pltpu.make_async_remote_copy(spart.at[peer], srecv.at[s], ssend, srec, device_id={"side": peer}, device_id_type=MESH)
        c.start()
        scopies.append(c)
    for n in range(4):
        xs = jnp.dot(pick, ubuf[:, COLS * n:COLS * n + COLS], preferred_element_type=F32).astype(BF)
        xbuf[:, COLS * n:COLS * n + COLS] = xs

    peers = [((d + k // 4) % 4, (s + k % 4) % 4) for k in range(16)]
    low = (iota((32, 256), 0) & 7) < 4

    def row_copy(p, k):
        pd, ps = peers[k]
        return pltpu.make_async_remote_copy(ybuf.at[4 * pd + ps, p], rbuf.at[4 * d + s, p], rsend, rrecv,
                                            device_id={"dev": pd, "side": ps}, device_id_type=MESH)

    def unit_body(p, carry):
        slot0 = (2 * p + 2) % NA
        slot1 = (2 * p + 3) % NA
        slotb = (p + 1) % NB
        pltpu.make_async_copy(wg.at[0, 0], abuf.at[slot0], asem.at[slot0]).wait()
        pltpu.make_async_copy(wu.at[0, 0], abuf.at[slot1], asem.at[slot1]).wait()
        inner(xbuf[pl.ds(pl.multiple_of(p * 32, 32), 32), :], slot0, slot1, chunks)

        @pl.when(p == 0)
        def _():
            a_copy(7).start()
            a_copy(8).start()

        @pl.when(p == 1)
        def _():
            a_copy(9).start()

        pltpu.make_async_copy(wd.at[0, 0], bbuf.at[slotb], bsem.at[slotb]).wait()
        rows = hbuf[...]
        for n in range(4):
            left = jnp.dot(rows, bbuf[slotb, :, COLS * n:COLS * n + 256], preferred_element_type=F32)
            right = jnp.dot(rows, bbuf[slotb, :, COLS * n + 256:COLS * n + 512], preferred_element_type=F32)
            packed = jnp.where(low, left, right)
            for pd in range(4):
                ybuf[4 * pd + n, p] = packed[8 * pd:8 * pd + 8].astype(BF)
        for k in range(1, 16):
            row_copy(p, k).start()
        return carry

    lax.fori_loop(0, 4, unit_body, 0)

    rbuf[4 * d + s] = ybuf[4 * d + s]
    srecv[s] = spart[s]
    pltpu.make_async_copy(spart.at[0:3], spart.at[0:3], srec).wait()
    shared = (srecv[0] + srecv[1] + srecv[2] + srecv[3]).astype(BF).astype(F32)
    pltpu.make_async_copy(ybuf.at[0:15], ybuf.at[0:15], rrecv).wait()
    got = jnp.dot(stackv[...], rbuf[...].reshape(512, 256), preferred_element_type=F32)
    routed = jnp.concatenate([got[0:32] + got[32:64] + got[64:96], got[96:128] + got[128:160] + got[160:192]], axis=1)
    obuf[...] = (mid.astype(F32) + shared + routed).astype(BF)
    ocopies = [pltpu.make_async_remote_copy(obuf, out.at[:, col], osend, orecv,
                                            device_id={"side": (s + k) % 4}, device_id_type=MESH) for k in range(1, 4)]
    for c in ocopies:
        c.start()
    mine = pltpu.make_async_copy(obuf, out.at[:, col], olocal)
    mine.start()

    pltpu.make_async_copy(cbuf.at[0:3], cbuf.at[0:3], csend).wait()
    pltpu.make_async_copy(idsx.at[0:3], idsx.at[0:3], isend).wait()
    pltpu.make_async_copy(mbuf.at[0:15], mbuf.at[0:15], msend).wait()
    pltpu.make_async_copy(spart.at[0:3], spart.at[0:3], ssend).wait()
    pltpu.make_async_copy(ybuf.at[0:15], ybuf.at[0:15], rsend).wait()
    pltpu.make_async_copy(cbuf.at[0:3], cbuf.at[0:3], osend).wait()
    mine.wait()
    pltpu.make_async_copy(cbuf.at[0:3], cbuf.at[0:3], orecv).wait()


def solution(mesh):
    def device_fn(hidden, k_cache, v_cache, cache_lens, expert_ids, route_gates, *weights):
        any_spec = pl.BlockSpec(memory_space=pl.ANY)
        dma = pltpu.SemaphoreType.DMA
        vm = pltpu.VMEM
        return pl.pallas_call(
            kernel,
            out_shape=jax.ShapeDtypeStruct((ROWS, DIM), BF),
            in_specs=[any_spec] * 17,
            out_specs=any_spec,
            scratch_shapes=[
                vm((ROWS, DIM), BF), vm((ROWS, COLS), BF), vm((1, ROWS), jnp.int32), vm((4, ROWS), jnp.int32),
                vm((4, ROWS), F32), vm((1, DIM), F32), vm((1, DIM), F32),
                vm((ROWS, HEADS, 128, 128), BF), vm((ROWS, HEADS, 128, 128), BF),
                vm((NA, DIM, FF), BF), vm((NB, FF, DIM), BF),
                vm((4, 8, 128), F32), vm((4, ROWS, COLS), BF), vm((16, ROWS, COLS), BF),
                vm((128, DIM), BF), vm((128, DIM), BF), vm((ROWS, FF), BF),
                vm((16, 4, 8, 256), BF), vm((16, 4, 8, 256), BF),
                vm((4, ROWS, COLS), F32), vm((4, ROWS, COLS), F32), vm((ROWS, COLS), BF), vm((192, 512), BF),
                dma((7,)), dma((6,)), dma((NA,)), dma((NB,)), dma, dma, dma, dma, dma, dma((3,)), dma((4,)), dma((4,)), dma((4,)),
                dma, dma, dma, dma, dma, dma, dma,
            ],
            compiler_params=pltpu.CompilerParams(collective_id=0, has_side_effects=True, vmem_limit_bytes=67000000),
            name="moe_decode",
        )(hidden, k_cache, v_cache, cache_lens.reshape(1, ROWS), jnp.swapaxes(expert_ids, 1, 2),
          jnp.swapaxes(route_gates, 1, 2), *weights)

    batch = P(("inst", "dev"))
    layer = P(None, ("inst", "dev"))
    expert = P(None, "dev")
    in_specs = (batch, layer, layer, batch, layer, layer) + (P(),) * 8 + (expert,) * 3
    return jax.shard_map(device_fn, mesh=mesh, in_specs=in_specs, out_specs=batch, check_vma=False)
```

time: 57.3 us -> 47.2 us (0.82)
  Pallas kernels: 52.9 us -> 45.5 us
  local copies, waits for them, and re-layouts: 4.29 us -> 1.57 us
    pallas_call x1, Pallas kernels: 52.9 us -> 45.5 us  [device_fn(): pl.pallas_call(kernel, out_shape=jax.ShapeDtypeStruct((ROWS, DIM), BF), i...]
    unnamed x3 -> x1, local copies, waits for them, and re-layouts: 4.29 us -> 1.57 us
where the time goes in v2:
time: 47.2 us; the launch traced here: 47.1 us
  Pallas kernels  45.5 us (96%)
  local copies, waits for them, and re-layouts  1.57 us (3%)
    pallas_call x1, Pallas kernels, device_fn(): pl.pallas_call(kernel, out_shape=jax.ShapeDtypeStruct((ROWS, DIM), BF), i...  45.5 us
    unnamed x1, local copies, waits for them, and re-layouts  1.57 us

profile of v2, /device:TPU:0, one launch (start us, length us, event | category | flops | bytes accessed | tf_op | source)
XLA Modules:
  0.0 47.1 jit_solution(13567797271430518570)
XLA Ops:
  0.0 45.5 %moe_decode.1 = bf16[32,2048]{1,0:T(8,128)(2,1)} custom-call(bf16[32,2048]{1,0:T(8,128)(2,1)} %hid.1, bf16[1,32,16,128,128]{4,3,2,1,0:T(8,128)(2,1)} %kc.1, bf16[1,32,16,128,128]{4,3,2,1,0:T(8,128)(2,1)} %vc.1, s32[1,32]{1,0:T(1,128)} %bitcast.5, s32[1,4,32]{2,1,0:T(4,128)} %bitcast.3, f32[1,4,32]{2,1,0:T(4,128)} %bitcast.4, f32[1,2048]{1,0:T(1,128)} %ga.1, ...), custom_call_target="tpu_custom_call" | custom-call | tf_op jit(solution)/shard_map/moe_decode/pallas_call | solution.py:381
  45.5 1.6 %copy.19 = bf16[32,2048]{1,0:T(8,128)(2,1)} copy(bf16[32,2048]{1,0:T(8,128)(2,1)} %moe_decode.1) | data formatting | bytes 262144

commit v3 on v2

v3 whole, which is shorter than its diff:
```python
import functools
import math

import jax
import jax.numpy as jnp
from jax import lax
from jax.experimental import pallas as pl
from jax.experimental.pallas import tpu as pltpu
from jax.sharding import PartitionSpec as P

NORM_EPS = 1e-6
ROPE_BASE = 10000.0
MESH = pl.DeviceIdType.MESH
BF = jnp.bfloat16
F32 = jnp.float32

ROWS = 32
COLS = 512
HEADS = 4
DIM = 2048
FF = 1408
SPLIT = 1024
TAIL = 1152
NA = 5
NB = 4


def rms(rows_f, gain):
    inv = lax.rsqrt(jnp.mean(rows_f * rows_f, axis=-1, keepdims=True) + NORM_EPS)
    return (rows_f * inv * gain).astype(BF)


class Load:
    def __init__(self, src, dst, sem, pieces=4):
        rows = dst.shape[0] // pieces
        self.whole = (src, dst, sem)
        self.pieces = [(src.at[rows * n:rows * n + rows], dst.at[rows * n:rows * n + rows], sem) for n in range(pieces)]

    def start(self):
        for c in self.pieces:
            pltpu.make_async_copy(*c).start()

    def wait(self):
        pltpu.make_async_copy(*self.whole).wait()


def arrived(ref, blocks, sem):
    pltpu.make_async_copy(ref.at[:blocks], ref.at[:blocks], sem).wait()


def span(n, width):
    return slice(width * n, width * n + width)


def flag(condition):
    return jnp.where(condition, 1.0, 0.0)


def row_id(shape):
    return lax.broadcasted_iota(jnp.int32, shape, 0)


def col_id(shape):
    return lax.broadcasted_iota(jnp.int32, shape, 1)


def silu(v):
    return v * jax.nn.sigmoid(v)


def kernel(hid, kc, vc, lens, ids, gts, ga, gf, wq, wkv, wo, sg, su, sd, wg, wu, wd, out,
           hidv, hidc, lensv, idsv, gtsv, gav, gfv, kb, vb, abuf, bbuf,
           idsx, cbuf, mbuf, ubuf, xbuf, hbuf, ybuf, rbuf, spart, srecv, stackv,
           sm, wsem, asem, bsem, isend, irecv, csend, crecv, msend, zrecv, yrecv, drecv, erecv,
           rsend, rrecv, ssend, srec, osend, orecv):
    d = lax.axis_index("dev")
    s = lax.axis_index("side")
    col = pl.ds(pl.multiple_of(s * COLS, COLS), COLS)

    kc, vc, ids, gts, wq, wkv, wo, sg, su, sd, wg, wu, wd = (ref.at[0] for ref in (kc, vc, ids, gts, wq, wkv, wo, sg, su, sd, wg, wu, wd))
    small = [(hid, hidv), (hid.at[:, col], hidc), (lens, lensv), (ids, idsv), (gts, gtsv), (ga, gav), (gf, gfv)]
    small = [pltpu.make_async_copy(a, b, sm.at[n]) for n, (a, b) in enumerate(small)]
    for c in small:
        c.start()
    vcol = pl.ds(pl.multiple_of(DIM + s * COLS, COLS), COLS)
    wqv, wkv_k, wkv_v, wob = abuf.at[3, :, 0:512], abuf.at[3, :, 512:1024], abuf.at[4, :, 0:512], abuf.at[4, :, 512:1024]
    big = [(wq.at[:, col], wqv), (wkv.at[:, col], wkv_k), (wkv.at[:, vcol], wkv_v),
           (kc.at[:, pl.ds(s * HEADS, 2)], kb.at[:, 0:2]), (vc.at[:, pl.ds(s * HEADS, 2)], vb.at[:, 0:2]), (wo.at[:, col], wob),
           (kc.at[:, pl.ds(s * HEADS + 2, 2)], kb.at[:, 2:4]), (vc.at[:, pl.ds(s * HEADS + 2, 2)], vb.at[:, 2:4])]
    big = [pltpu.make_async_copy(a, b, wsem.at[n]) for n, (a, b) in enumerate(big)]
    for n in range(3):
        big[n].start()

    barrier = pltpu.get_barrier_semaphore()
    for k in range(1, 16):
        peer = {"dev": (d + k // 4) % 4, "side": (s + k % 4) % 4}
        pl.semaphore_signal(barrier, inc=1, device_id=peer, device_id_type=MESH)

    last = s == 3
    front = jnp.logical_not(last)
    shift = jnp.where(last, 1, 0)
    head = pl.ds(pl.multiple_of(s * SPLIT, SPLIT), SPLIT)
    body = pl.ds(3 * SPLIT, FF)
    rest = pl.ds(3 * SPLIT + FF, TAIL)

    def local_expert(p):
        return 4 * s + p - shift

    def a_expert(n):
        slot = n % NA
        return Load((wg, wu)[n % 2].at[local_expert(n // 2 - 1)], abuf.at[slot], asem.at[slot])

    def a_shared(n, part):
        width = {SPLIT: head, FF: body, TAIL: rest}[part]
        return Load((sg, su)[n % 2].at[:, width], abuf.at[n, :, 0:part], asem.at[n])

    def b_expert(n):
        slot = n % NB
        return Load(wd.at[local_expert(n - 1)], bbuf.at[slot], bsem.at[slot])

    def b_shared(n, part):
        width = {SPLIT: head, FF: body, TAIL: rest}[part]
        return Load(sd.at[width], bbuf.at[n, 0:part], bsem.at[n])

    for n in range(16):
        ybuf[n, 0] = jnp.zeros((8, 256), BF)
    for c in small:
        c.wait()
    big[3].start()
    big[6].start()
    normed = rms(hidv[...].astype(F32), gav[...])
    lens_row = lensv[...].astype(F32)
    eye = row_id((ROWS, ROWS)) == col_id((ROWS, ROWS))
    lens_col = jnp.sum(jnp.where(eye, jnp.broadcast_to(lens_row, (ROWS, ROWS)), 0.0), axis=1, keepdims=True)
    lane = col_id((ROWS, 128))
    freq = jnp.exp((lane & 63).astype(F32) * (-2.0 * math.log(ROPE_BASE) / 128.0))
    angle = lens_col * freq
    cosine = jnp.cos(angle)
    sine = jnp.where(lane < 64, -jnp.sin(angle), jnp.sin(angle))

    def rope(v):
        return (v * cosine + pltpu.roll(v, 64, axis=1) * sine).astype(BF).astype(F32)

    idf = idsv[...].astype(F32)
    wide_ids = jnp.concatenate([idf] * 4, axis=1)
    idsx[d, 0:4, :] = jnp.where(col_id((4, 128)) >> 5 == d, wide_ids, 0.0)
    idsx[d, 4:8, :] = jnp.zeros((4, 128), F32)

    big[0].wait()
    big[4].start()
    big[7].start()
    q_all = jnp.dot(normed, wqv[...], preferred_element_type=F32).astype(BF).astype(F32)
    big[1].wait()
    big[5].start()

    @pl.when(last)
    def _():
        a_shared(0, FF).start()
        a_shared(1, FF).start()
        b_shared(0, FF).start()

    @pl.when(front)
    def _():
        a_shared(0, SPLIT).start()
        a_shared(1, SPLIT).start()
        b_shared(0, SPLIT).start()

    k_all = jnp.dot(normed, wkv_k[...], preferred_element_type=F32).astype(BF).astype(F32)
    big[2].wait()
    v_all = jnp.dot(normed, wkv_v[...], preferred_element_type=F32).astype(BF).astype(F32)

    @pl.when(last)
    def _():
        a_shared(2, TAIL).start()
        a_shared(3, TAIL).start()
        b_shared(1, TAIL).start()

    @pl.when(front)
    def _():
        a_expert(2).start()
        a_expert(3).start()
        b_expert(1).start()

    b_expert(2).start()
    b_expert(3).start()

    q_h = [rope(q_all[:, span(h, 128)]) for h in range(HEADS)]
    k_h = [rope(k_all[:, span(h, 128)]) for h in range(HEADS)]
    v_h = [v_all[:, span(h, 128)] for h in range(HEADS)]

    row8 = row_id((8, 128))
    big[3].wait()
    parts = []
    for h in range(HEADS):
        if h == 2:
            big[6].wait()
        for g in range(4):
            q8 = q_h[h][span(g, 8)].astype(BF)
            keys = kb[span(g, 8), h].reshape(8 * 128, 128)
            full = lax.dot_general(q8, keys, (((1,), (1,)), ((), ())), preferred_element_type=F32)
            acc = jnp.zeros((8, 128), F32)
            for t in range(8):
                acc = acc + jnp.where(row8 == t, full[:, span(t, 128)], 0.0)
            parts.append(acc)
    scale = 128 ** -0.5
    scores = jnp.concatenate(parts, axis=0) * scale
    q_cat = jnp.concatenate(q_h, axis=0)
    k_cat = jnp.concatenate(k_h, axis=0)
    v_cat = jnp.concatenate(v_h, axis=0)
    lens_cat = jnp.concatenate([lens_col] * HEADS, axis=0)
    scores = jnp.where(col_id((128, 128)).astype(F32) < lens_cat, scores, -jnp.inf)
    self_score = jnp.sum(q_cat * k_cat, axis=1, keepdims=True) * scale
    peak = jnp.maximum(jnp.max(scores, axis=1, keepdims=True), self_score)
    weights = jnp.exp(scores - peak)
    self_weight = jnp.exp(self_score - peak)
    denom = jnp.sum(weights, axis=1, keepdims=True) + self_weight
    prob = (weights / denom).astype(BF).astype(F32)
    self_prob = (self_weight / denom).astype(BF).astype(F32)
    big[4].wait()
    for h in range(HEADS):
        if h == 2:
            big[7].wait()
        ctx = []
        for g in range(4):
            n = 4 * h + g
            p8 = prob[span(n, 8)]
            wide = jnp.concatenate([jnp.where(row8 == t, p8, 0.0) for t in range(8)], axis=1).astype(BF)
            vals = vb[span(g, 8), h].reshape(8 * 128, 128)
            ctx.append(jnp.dot(wide, vals, preferred_element_type=F32))
        ctx = jnp.concatenate(ctx, axis=0)
        ctx = ctx + self_prob[span(h, 32)] * v_cat[span(h, 32)]
        cbuf[s, :, span(h, 128)] = ctx.astype(BF)

    pl.semaphore_wait(barrier, 15)
    ccopies = []
    for k in range(1, 4):
        c = pltpu.make_async_remote_copy(cbuf.at[s], cbuf.at[s], csend, crecv,
                                         device_id={"side": (s + k) % 4}, device_id_type=MESH)
        c.start()
        ccopies.append(c)
    icopies = []
    for k in range(1, 4):
        c = pltpu.make_async_remote_copy(idsx.at[d], idsx.at[d], isend, irecv,
                                         device_id={"dev": (d + k) % 4}, device_id_type=MESH)
        c.start()
        icopies.append(c)

    lanes = 512
    l = col_id((ROWS, lanes))
    tok = row_id((ROWS, lanes))
    lside = (l >> 5) & 3
    lunit = (l >> 3) & 3
    lexp = 15 * (l >> 7) + 4 * lside + lunit - jnp.where(lside == 3, 1, 0)
    lexp = jnp.where(jnp.logical_and(lside == 3, lunit == 0), -1, lexp).astype(F32)
    hits = jnp.zeros((ROWS, lanes), F32)
    gated = jnp.zeros((ROWS, lanes), F32)
    gates = gtsv[...]

    def column(row):
        return jnp.sum(jnp.where(eye, jnp.broadcast_to(row, (ROWS, ROWS)), 0.0), axis=1, keepdims=True)

    for j in range(4):
        same = jnp.broadcast_to(column(idf[j:j + 1]), (ROWS, lanes)) == lexp
        hits = hits + flag(same)
        gated = gated + jnp.where(same, jnp.broadcast_to(column(gates[j:j + 1]), (ROWS, lanes)), 0.0)
    a0 = row_id((ROWS, ROWS))
    a1 = col_id((ROWS, ROWS))
    before = flag(jnp.logical_and(a0 >> 4 == a1 >> 4, a1 < a0)).astype(BF)
    order = jnp.dot(before, hits.astype(BF), preferred_element_type=F32)
    fits = jnp.logical_and(order == (l & 1).astype(F32), (tok >> 4) == ((l >> 1) & 1))
    gated = jnp.where(fits, gated, 0.0)
    stack = []
    for half in range(2):
        g = jnp.where(((l >> 2) & 1) == half, gated, 0.0)
        for _ in range(3):
            piece = g.astype(BF)
            stack.append(piece)
            g = g - piece.astype(F32)
    stackv[...] = jnp.concatenate(stack, axis=0)

    big[5].wait()
    arrived(cbuf, 3, crecv)
    mid = hidc[...].astype(F32)
    attn = jnp.zeros((ROWS, COLS), F32)
    for n in range(4):
        attn = attn + jnp.dot(cbuf[n], wob[span(n, COLS), :], preferred_element_type=F32)
    mid = (mid + attn).astype(BF)
    mbuf[4 * d + s] = mid
    a_expert(4).start()

    dx = (d, d + 1 - 2 * (d % 2), (d + 2) % 4, 3 - d)
    sx = (s, s + 1 - 2 * (s % 2), (s + 2) % 4, 3 - s)

    def tile_copy(plane, side, recv, peer):
        tile = mbuf.at[4 * plane + side]
        return pltpu.make_async_remote_copy(tile, tile, msend, recv, device_id=peer, device_id_type=MESH)

    inside = jnp.logical_or(d == 1, d == 2)
    code = (0, 1, jnp.where(inside, 3, 2), jnp.where(inside, 2, 3))
    near = (d, dx[1], jnp.where(inside, dx[3], dx[2]), jnp.where(inside, dx[2], dx[3]))
    zc = [None] + [tile_copy(d, s, zrecv.at[code[k]], {"dev": near[k]}) for k in range(1, 4)]
    yc = [tile_copy(near[q], s, yrecv.at[q], {"side": sx[2]}) for q in range(4)]
    dc = [tile_copy(near[q], s, drecv.at[q], {"side": sx[1]}) for q in range(4)]
    ec = [tile_copy(near[q], sx[2], erecv.at[q], {"side": sx[1]}) for q in range(4)]

    def from_z(k):
        zc[k].wait_recv()
        yc[k].start()
        dc[k].start()

    def from_y(q):
        yc[q].wait_recv()
        ec[q].start()

    def norm_plane(q):
        dc[q].wait_recv()
        ec[q].wait_recv()
        rows = jnp.concatenate([mbuf[4 * near[q] + n] for n in range(4)], axis=1).astype(F32)
        u = rms(rows, gfv[...])
        ubuf[pl.ds(pl.multiple_of(near[q] * ROWS, ROWS), ROWS), :] = u


    for k in range(1, 4):
        zc[k].start()
    yc[0].start()
    dc[0].start()

    chunks = [(256 * n, 256) for n in range(5)] + [(1280, 128)]

    def inner(rows, slot0, slot1, part):
        for off, width in part:
            gate = jnp.dot(rows, abuf[slot0, :, off:off + width], preferred_element_type=F32)
            up = jnp.dot(rows, abuf[slot1, :, off:off + width], preferred_element_type=F32)
            hbuf[:, off:off + width] = (silu(gate) * up).astype(BF)

    def shared_down(n):
        cols = slice(COLS * n, COLS * n + COLS)
        spart[n] = jnp.dot(hbuf[:, 0:SPLIT], bbuf[0, 0:SPLIT, cols], preferred_element_type=F32)

        @pl.when(last)
        def _():
            spart[n] = spart[n] + jnp.dot(hbuf[:, SPLIT:FF], bbuf[0, SPLIT:FF, cols], preferred_element_type=F32)


    from_y(0)
    arrived(idsx, 3, irecv)
    id_all = idsx[0] + idsx[1] + idsx[2] + idsx[3]
    r = row_id((64, 128))
    t = col_id((64, 128))
    unit = r >> 4
    expert = d * 15 + local_expert(unit)
    expert = jnp.where(jnp.logical_and(last, unit == 0), -1, expert).astype(F32)
    hit = jnp.zeros((64, 128), F32)
    for j in range(4):
        hit = hit + flag(jnp.broadcast_to(id_all[j:j + 1], (64, 128)) == expert)
    t0 = row_id((128, 128))
    t1 = col_id((128, 128))
    earlier = flag(jnp.logical_and(t0 >> 4 == t1 >> 4, t0 < t1)).astype(BF)
    rank = jnp.dot(hit.astype(BF), earlier, preferred_element_type=F32)
    place = jnp.logical_and(rank == (r & 1).astype(F32), t >> 4 == 2 * ((r >> 2) & 3) + ((r >> 1) & 1))
    pick = jnp.where(place, hit, 0.0).astype(BF)

    from_z(1)
    norm_plane(0)
    mine_rows = pl.ds(pl.multiple_of(d * ROWS, ROWS), ROWS)

    @pl.when(last)
    def _():
        a_shared(0, FF).wait()
        a_shared(1, FF).wait()

    @pl.when(front)
    def _():
        a_shared(0, SPLIT).wait()
        a_shared(1, SPLIT).wait()

    inner(ubuf[mine_rows, :], 0, 1, chunks[0:2])
    from_z(2)
    inner(ubuf[mine_rows, :], 0, 1, chunks[2:4])
    from_z(3)

    @pl.when(last)
    def _():
        inner(ubuf[mine_rows, :], 0, 1, chunks[4:6])

    a_expert(5).start()
    a_expert(6).start()

    @pl.when(last)
    def _():
        b_shared(0, FF).wait()

    @pl.when(front)
    def _():
        b_shared(0, SPLIT).wait()

    from_y(1)
    shared_down(0)
    from_y(2)
    shared_down(1)
    shared_down(2)
    from_y(3)
    shared_down(3)
    @pl.when(last)
    def _():
        a_shared(2, TAIL).wait()
        a_shared(3, TAIL).wait()
        inner(ubuf[mine_rows, :], 2, 3, chunks[0:4] + [(SPLIT, 128)])
        b_shared(1, TAIL).wait()
        for n in range(4):
            spart[n] = spart[n] + jnp.dot(hbuf[:, 0:TAIL], bbuf[1, 0:TAIL, span(n, COLS)], preferred_element_type=F32)

    for q in range(1, 4):
        norm_plane(q)
    for k in range(1, 4):
        peer = (s + k) % 4
        pltpu.make_async_remote_copy(spart.at[peer], srecv.at[s], ssend, srec, device_id={"side": peer}, device_id_type=MESH).start()
    for n in range(4):
        xs = jnp.dot(pick, ubuf[:, span(n, COLS)], preferred_element_type=F32).astype(BF)
        xbuf[:, span(n, COLS)] = xs

    low = row_id((8, 256)) < 4

    def row_copy(p, pd, ps):
        return pltpu.make_async_remote_copy(ybuf.at[4 * pd + ps, p], rbuf.at[4 * d + s, p], rsend, rrecv,
                                            device_id={"dev": pd, "side": ps}, device_id_type=MESH)

    def send_rows(p, hop, first):
        for q in (2, 3, 1, 0):
            for side in ((s + 1) % 2, s % 2):
                if hop or q:
                    row_copy(p, dx[q], first + side).start()
        if not hop:
            row_copy(p, d, sx[1]).start()

    def unit_body(p, carry):
        slot0 = (2 * p + 2) % NA
        slot1 = (2 * p + 3) % NA
        slotb = (p + 1) % NB
        is_rest = jnp.logical_and(last, p == 0)

        @pl.when(jnp.logical_not(is_rest))
        def _():
            pltpu.make_async_copy(wg.at[0], abuf.at[slot0], asem.at[slot0]).wait()
            pltpu.make_async_copy(wu.at[0], abuf.at[slot1], asem.at[slot1]).wait()

            rows = xbuf[pl.ds(pl.multiple_of(p * 16, 16), 16), :]
            gate = jnp.dot(rows, abuf[slot0], preferred_element_type=F32)
            up = jnp.dot(rows, abuf[slot1], preferred_element_type=F32)
            hbuf[0:16, :] = (silu(gate) * up).astype(BF)

        @pl.when(p == 0)
        def _():
            a_expert(7).start()
            a_expert(8).start()

        @pl.when(p == 1)
        def _():
            a_expert(9).start()

        @pl.when(p == 2)
        def _():
            b_expert(4).start()

        @pl.when(is_rest)
        def _():
            for hop in (2, 0):
                send_rows(p, hop, (s - s % 2 + hop) % 4)

        @pl.when(jnp.logical_not(is_rest))
        def _():
            pltpu.make_async_copy(wd.at[0], bbuf.at[slotb], bsem.at[slotb]).wait()

            rows = hbuf[0:16, :]
            for hop in (2, 0):
                first = (s - s % 2 + hop) % 4
                res = jnp.dot(rows, bbuf[slotb, :, pl.ds(pl.multiple_of(first * COLS, 2 * COLS), 2 * COLS)], preferred_element_type=F32)
                for side in range(2):
                    for pair in range(2):
                        left = res[span(pair, 8), COLS * side:COLS * side + 256]
                        right = res[span(pair, 8), COLS * side + 256:COLS * side + 512]
                        even = jnp.where(low, left, pltpu.roll(right, 4, axis=0))
                        odd = jnp.where(low, pltpu.roll(left, 4, axis=0), right)
                        ybuf[8 * pair + first + side, p] = even.astype(BF)
                        ybuf[8 * pair + 4 + first + side, p] = odd.astype(BF)
                send_rows(p, hop, first)

        return carry

    lax.fori_loop(0, 4, unit_body, 0)

    rbuf[4 * d + s] = ybuf[4 * d + s]
    srecv[s] = spart[s]
    arrived(spart, 3, srec)
    shared = (srecv[0] + srecv[1] + srecv[2] + srecv[3]).astype(BF).astype(F32)
    arrived(ybuf, 15, rrecv)
    got = jnp.dot(stackv[...], rbuf[...].reshape(512, 256), preferred_element_type=F32)
    got = [got[span(n, ROWS)] for n in range(6)]
    routed = jnp.concatenate([got[0] + got[1] + got[2], got[3] + got[4] + got[5]], axis=1)
    out[:, col] = (mid.astype(F32) + shared + routed).astype(BF)
    ocopies = [pltpu.make_async_remote_copy(out.at[:, col], out.at[:, col], osend, orecv,
                                            device_id={"side": (s + k) % 4}, device_id_type=MESH) for k in range(1, 4)]
    for c in ocopies:
        c.start()

    arrived(cbuf, 3, csend)
    arrived(idsx, 3, isend)
    arrived(mbuf, 15, msend)
    arrived(spart, 3, ssend)
    arrived(ybuf, 15, rsend)
    arrived(cbuf, 3, osend)
    arrived(cbuf, 3, orecv)


def solution(mesh):
    def device_fn(hidden, k_cache, v_cache, cache_lens, expert_ids, route_gates, *weights):
        any_spec = pl.BlockSpec(memory_space=pl.ANY)
        dma = pltpu.SemaphoreType.DMA
        vm = pltpu.VMEM
        return pl.pallas_call(
            kernel,
            out_shape=pltpu.VMEM((ROWS, DIM), BF),
            in_specs=[any_spec] * 17,
            out_specs=pl.BlockSpec(memory_space=pltpu.VMEM),
            scratch_shapes=[
                vm((ROWS, DIM), BF), vm((ROWS, COLS), BF), vm((1, ROWS), jnp.int32), vm((4, ROWS), jnp.int32),
                vm((4, ROWS), F32), vm((1, DIM), F32), vm((1, DIM), F32),
                vm((ROWS, HEADS, 128, 128), BF), vm((ROWS, HEADS, 128, 128), BF),
                vm((NA, DIM, FF), BF), vm((NB, FF, DIM), BF),
                vm((4, 8, 128), F32), vm((4, ROWS, COLS), BF), vm((16, ROWS, COLS), BF),
                vm((128, DIM), BF), vm((64, DIM), BF), vm((ROWS, FF), BF),
                vm((16, 4, 8, 256), BF), vm((16, 4, 8, 256), BF),
                vm((4, ROWS, COLS), F32), vm((4, ROWS, COLS), F32), vm((192, 512), BF),
                dma((7,)), dma((8,)), dma((NA,)), dma((NB,)), dma, dma, dma, dma, dma, dma((4,)), dma((4,)), dma((4,)), dma((4,)),
                dma, dma, dma, dma, dma, dma,
            ],
            compiler_params=pltpu.CompilerParams(collective_id=0, has_side_effects=True, vmem_limit_bytes=66000000),
            name="moe_decode",
        )(hidden, k_cache, v_cache, cache_lens.reshape(1, ROWS), jnp.swapaxes(expert_ids, 1, 2),
          jnp.swapaxes(route_gates, 1, 2), *weights)

    batch = P(("inst", "dev"))
    layer = P(None, ("inst", "dev"))
    expert = P(None, "dev")
    in_specs = (batch, layer, layer, batch, layer, layer) + (P(),) * 8 + (expert,) * 3
    return jax.shard_map(device_fn, mesh=mesh, in_specs=in_specs, out_specs=batch, check_vma=False)
```

time: 47.2 us -> 42.4 us (0.90)
  Pallas kernels: 45.5 us -> 41.6 us
  local copies, waits for them, and re-layouts: 1.57 us -> 0.66 us
    pallas_call x1, Pallas kernels: 45.5 us -> 41.6 us  [device_fn(): pl.pallas_call(kernel, out_shape=pltpu.VMEM((ROWS, DIM), BF), in_specs=[a...]
    unnamed x1, local copies, waits for them, and re-layouts: 1.57 us -> 0.66 us
where the time goes in v3:
time: 42.4 us; the launch traced here: 42.2 us
  Pallas kernels  41.6 us (98%)
  local copies, waits for them, and re-layouts  0.66 us (2%)
    pallas_call x1, Pallas kernels, device_fn(): pl.pallas_call(kernel, out_shape=pltpu.VMEM((ROWS, DIM), BF), in_specs=[a...  41.6 us

profile of v3, /device:TPU:0, one launch (start us, length us, event | category | flops | bytes accessed | tf_op | source)
XLA Modules:
  0.0 42.2 jit_solution(13264599465237465582)
XLA Ops:
  0.0 41.6 %moe_decode.1 = bf16[32,2048]{1,0:T(8,128)(2,1)S(1)} custom-call(bf16[32,2048]{1,0:T(8,128)(2,1)} %hid.1, bf16[1,32,16,128,128]{4,3,2,1,0:T(8,128)(2,1)} %kc.1, bf16[1,32,16,128,128]{4,3,2,1,0:T(8,128)(2,1)} %vc.1, s32[1,32]{1,0:T(1,128)} %bitcast.5, s32[1,4,32]{2,1,0:T(4,128)} %bitcast.3, f32[1,4,32]{2,1,0:T(4,128)} %bitcast.4, f32[1,2048]{1,0:T(1,128)} %ga.1, ...), custom_call_target="tpu_custom_call" | custom-call | tf_op jit(solution)/shard_map/moe_decode/pallas_call | solution.py:520
  41.6 0.7 %copy.19 = bf16[32,2048]{1,0:T(8,128)(2,1)} copy(bf16[32,2048]{1,0:T(8,128)(2,1)S(1)} %moe_decode.1) | data formatting | bytes 262144
